TPU v7x, 32 devices: a whole 2x2x4 slice. The times are simulated.
32 devices in a mesh: rep: 8 (over z, core), tp: 4 (over y, x).
Axes of the slice: x: 2, y: 2, z: 4, core: 2. Of those that a mesh axis runs over, the one named last changes fastest.
Arguments:
- hidden: bfloat16 [32, 4608], P('rep'), may hold values from -6 to 6
- positions: int32 [32], P('rep'), may hold values from 1 to 1023
- key_cache: bfloat16 [32, 16, 1024, 128], P('rep', 'tp'), may hold values from -6 to 6
- value_cache: bfloat16 [32, 16, 1024, 128], P('rep', 'tp'), may hold values from -6 to 6
- norm_gain: float32 [4608], replicated, may hold values from 0.1 to 1.9
- q_proj: bfloat16 [4096, 4608], P(('rep', 'tp')), may hold values from -0.09375 to 0.09375
- k_proj: bfloat16 [2048, 4608], P(('rep', 'tp')), may hold values from -0.09375 to 0.09375
- v_proj: bfloat16 [2048, 4608], P(('rep', 'tp')), may hold values from -0.09375 to 0.09375
- o_proj: bfloat16 [4608, 4096], P(('rep', 'tp')), may hold values from -0.09375 to 0.09375
- post_gain: float32 [4608], P('tp'), may hold values from 0.1 to 1.9
Outputs:
- joined_qkv: bfloat16 [4608, 8192], P(None, 'tp')
- wo_heads: bfloat16 [4096, 4608], P('tp')
- attn_out: bfloat16 [32, 4608], P('rep', 'tp')
All inputs are finite; a program needn't handle non-finite values.
Results may differ from a plain program's by a relative error of at most 0.008.
Values may be sent and summed in bfloat16 or wider, within the bound.
A program may use at most 128 MiB of HBM per device.

v0:
```python
import functools

import jax
import jax.numpy as jnp
from jax import lax
from jax.experimental import pallas as pl
from jax.experimental.pallas import tpu as pltpu
from jax.sharding import PartitionSpec as P

score_scale = 144.0 ** (-0.5)
soft_cap = 50.0


def rms_scale(values, gain):
    mean_square = jnp.mean(values * values, axis=-1, keepdims=True)
    return values * lax.rsqrt(mean_square + 1e-06) * gain


def rotate(values, positions):
    half = values.shape[-1] // 2
    freq = 10000.0 ** (-2.0 * jnp.arange(half, dtype=jnp.float32) / values.shape[-1])
    angle = positions.astype(jnp.float32)[:, None] * freq[None, :]
    cosine = jnp.cos(angle)[:, None, :]
    sine = jnp.sin(angle)[:, None, :]
    first = values[..., :half]
    second = values[..., half:]
    return jnp.concatenate(
        [first * cosine - second * sine, second * cosine + first * sine], axis=-1
    )


def join_kernel(per_tp, q_rows, k_rows, *refs):
    slot = lax.rem(lax.axis_index("rep"), per_tp)
    parts, out_ref = refs[:-1], refs[-1]
    tp_count = parts[0].shape[0]
    q_all = tp_count * per_tp * q_rows
    k_all = tp_count * per_tp * k_rows
    for step in range(per_tp):
        who = lax.rem(slot + step, per_tp)
        q_ref, kv_ref = parts[2 * step], parts[2 * step + 1]
        for start, ref, low, rows in (
            (0, q_ref, 0, q_rows),
            (q_all, kv_ref, 0, k_rows),
            (q_all + k_all, kv_ref, k_rows, k_rows),
        ):
            block = ref[:, low : low + rows, :].reshape(tp_count * rows, -1)
            at = pl.multiple_of(start + who * (tp_count * rows), 128)
            out_ref[:, pl.ds(at, tp_count * rows)] = jnp.transpose(block)


def join(per_tp, pairs):
    tp_count, q_rows, width = pairs[0][0].shape
    k_rows = pairs[0][1].shape[1] // 2
    columns = tp_count * per_tp * (q_rows + 2 * k_rows)
    stripe = 256
    operands, specs = [], []
    for pair in pairs:
        for matrix in pair:
            operands.append(matrix)
            specs.append(
                pl.BlockSpec((tp_count, matrix.shape[1], stripe), lambda j: (0, 0, j))
            )
    size = width * columns * 2
    return pl.pallas_call(
        functools.partial(join_kernel, per_tp, q_rows, k_rows),
        grid=(width // stripe,),
        in_specs=specs,
        out_specs=pl.BlockSpec((stripe, columns), lambda j: (j, 0)),
        out_shape=jax.ShapeDtypeStruct((width, columns), jnp.bfloat16),
        cost_estimate=pl.CostEstimate(flops=0, bytes_accessed=2 * size, transcendentals=0),
        name="join",
    )(*operands)


def turn_kernel(rows_ref, out_ref):
    out_ref[...] = jnp.transpose(rows_ref[...])


def turn(rows):
    height, width = rows.shape
    stripe = 384 if height % 384 == 0 else 128
    return pl.pallas_call(
        turn_kernel,
        grid=(height // stripe,),
        in_specs=[pl.BlockSpec((stripe, width), lambda j: (j, 0))],
        out_specs=pl.BlockSpec((width, stripe), lambda j: (0, j)),
        out_shape=jax.ShapeDtypeStruct((width, height), rows.dtype),
        cost_estimate=pl.CostEstimate(
            flops=0, bytes_accessed=4 * height * width, transcendentals=0
        ),
        name="turn",
    )(rows)


def body(
    hidden, positions, key_cache, value_cache, norm_gain, q_proj, k_proj, v_proj, o_proj, post_gain
):
    tp_count = lax.axis_size("tp")
    replica_count = lax.axis_size("rep")
    per_tp = replica_count // tp_count
    model_width = hidden.shape[1]
    q_rows, k_rows = q_proj.shape[0], k_proj.shape[0]

    groups = [[i + per_tp * p for p in range(tp_count)] for i in range(per_tp)]
    shifts = [
        [
            (per_tp * p + (i + d) % per_tp, per_tp * p + i)
            for p in range(tp_count)
            for i in range(per_tp)
        ]
        for d in range(1, per_tp)
    ]

    def collect(rows):
        planes = lax.all_gather(rows[None], "rep", axis=0, tiled=True, axis_index_groups=groups)
        return lax.all_to_all(planes, "tp", split_axis=0, concat_axis=0, tiled=True)

    kv_rows = collect(jnp.concatenate([k_proj, v_proj], axis=0))
    split_cols = o_proj.reshape(o_proj.shape[0], tp_count, -1)
    rows_of_group = lax.all_to_all(split_cols, "tp", split_axis=1, concat_axis=0, tiled=True)

    batch, kv_local, length, head_dim = key_cache.shape

    def scatter_rows(values):
        wide = values.reshape(replica_count, batch, -1)
        by_rep = lax.all_to_all(wide, "rep", split_axis=0, concat_axis=0, tiled=True)
        return by_rep

    def to_block(by_rep):
        arrived = lax.all_to_all(by_rep, "tp", split_axis=0, concat_axis=0, tiled=True)
        arrived = arrived.reshape(tp_count, per_tp, batch, -1)
        return jnp.transpose(arrived, (2, 1, 0, 3))

    normed = rms_scale(hidden.astype(jnp.float32), norm_gain).astype(jnp.bfloat16)
    normed_all = lax.all_gather(normed, "rep", axis=0, tiled=True)
    contract = (((1,), (1,)), ((), ()))
    local = jnp.concatenate(
        [
            lax.dot_general(normed_all, matrix, contract, preferred_element_type=jnp.float32)
            for matrix in (q_proj, k_proj, v_proj)
        ],
        axis=1,
    )
    block = to_block(scatter_rows(local))
    q_local = tp_count * per_tp * q_rows // head_dim
    group = q_local // kv_local
    query = block[..., :q_rows].reshape(batch, q_local, head_dim)
    keys_new = block[..., q_rows : q_rows + k_rows].reshape(batch, kv_local, head_dim)
    values_new = block[..., q_rows + k_rows :].reshape(batch, kv_local, head_dim)
    query_rot = rotate(query, positions).astype(jnp.bfloat16)
    rotated_keys = rotate(keys_new, positions).astype(jnp.bfloat16)
    values_rot = values_new.astype(jnp.bfloat16)
    grouped_heads = query_rot.reshape(batch, kv_local, group, head_dim)
    scores = (
        jnp.einsum("bkgd,bkld->bkgl", grouped_heads, key_cache, preferred_element_type=jnp.float32)
        * score_scale
    )
    capped = soft_cap * jnp.tanh(scores / soft_cap)
    valid = jnp.arange(length, dtype=jnp.int32)[None, :] < positions[:, None]
    weight_raw = jnp.where(valid[:, None, None, :], jnp.exp(capped), 0.0)
    self_score = (
        jnp.einsum("juzy,juy->juz", grouped_heads, rotated_keys, preferred_element_type=jnp.float32)
        * score_scale
    )
    self_raw = jnp.exp(soft_cap * jnp.tanh(self_score / soft_cap))
    denom = jnp.sum(weight_raw, axis=-1) + self_raw
    weights = (weight_raw / denom[..., None]).astype(jnp.bfloat16)
    self_weight = (self_raw / denom).astype(jnp.bfloat16)
    attention = jnp.einsum(
        "bkgl,bkld->bkgd", weights, value_cache, preferred_element_type=jnp.float32
    )
    attention = (
        attention
        + self_weight.astype(jnp.float32)[..., None] * values_rot.astype(jnp.float32)[:, :, None, :]
    )
    attention = attention.reshape(batch, q_local * head_dim).astype(jnp.bfloat16)
    q_later, attention = lax.optimization_barrier((q_proj, attention))
    q_own = collect(q_later)
    pairs = [(q_own, kv_rows)]
    for shift in shifts:
        pairs.append((lax.ppermute(q_own, "rep", shift), lax.ppermute(kv_rows, "rep", shift)))
    joined_block = join(per_tp, pairs)
    own_all = lax.all_gather(attention, "tp", axis=1, tiled=True)
    attention_all = lax.all_gather(own_all, "rep", axis=0, tiled=True)
    projected = lax.dot_general(
        attention_all, o_proj, contract, preferred_element_type=jnp.float32
    )
    by_rep = scatter_rows(projected)
    share = to_block(by_rep).reshape(batch, -1)
    square = jnp.sum(share * share, axis=1)
    square_all = lax.all_gather(square[None], "tp", axis=0, tiled=True)
    multiplier = lax.rsqrt(jnp.sum(square_all, axis=0) / model_width + 1e-06)
    result = share * multiplier[:, None] * post_gain
    rows_of_group, result = lax.optimization_barrier((rows_of_group, result))
    complete_rows = lax.all_gather(rows_of_group, "rep", axis=0, tiled=True)
    out_block = turn(complete_rows.reshape(model_width, -1))
    return (joined_block, out_block, result.astype(jnp.bfloat16))


def solution(mesh):
    in_specs = (
        P("rep", None),
        P("rep"),
        P("rep", "tp", None, None),
        P("rep", "tp", None, None),
        P(),
        P(("rep", "tp"), None),
        P(("rep", "tp"), None),
        P(("rep", "tp"), None),
        P(("rep", "tp"), None),
        P("tp"),
    )
    out_specs = (P(None, "tp"), P("tp", None), P("rep", "tp"))
    return jax.shard_map(body, mesh=mesh, in_specs=in_specs, out_specs=out_specs, check_vma=False)
```

profile of v0, /device:TPU:0, one launch (start us, length us, event | category | flops | bytes accessed | tf_op | source)
XLA Modules:
  0.0 305.3 jit_solution(17895576999306610099)
XLA Ops:
  7.2 0.0 all-gather.13.cloned.1.call-start
  7.3 2.5 pad_maximum_fusion
  9.7 0.0 all-gather.13.cloned.1.call-update
  9.8 0.9 fusion.5
  10.7 0.9 fusion.9
  11.6 16.5 %all-gather.3 = bf16[8,4,4608]{2,1,0:T(4,128)(2,1)S(1)} all-gather(bf16[1,4,4608]{2,1,0:T(4,128)(2,1)S(1)} %fusion.9), channel_id=1, replica_groups=mesh['rep'=8,'tp'=4] {'rep'}, dimensions={0}, use_global_device_ids=true | all-gather | bytes 331776 | tf_op jit(solution)/shard_map/all_gather | solution.py:135
  28.1 0.1 reshape.151
  28.2 0.3 fusion.17
  28.4 0.3 fusion.18
  28.7 0.0 copy-done.1
  28.7 0.5 fusion.16
  29.2 0.1 pad_maximum_fusion.1
  29.3 0.6 reshape.134
  29.9 5.2 %all-to-all-start = ((f32[8,4,256]{2,1,0:T(4,128)}), f32[8,4,256]{2,1,0:T(4,128)}, u32[]{:S(2)}, u32[]{:S(2)}) async-start(f32[8,4,256]{2,1,0:T(4,128)} %reshape.134), calls=%async_computation | async-start | bytes 65536 | tf_op jit(solution)/shard_map/all_to_all | solution.py:126
  35.1 0.1 multiply_cosine_fusion
  35.3 8.2 %all-to-all-done = f32[8,4,256]{2,1,0:T(4,128)} async-done(((f32[8,4,256]{2,1,0:T(4,128)}), f32[8,4,256]{2,1,0:T(4,128)}, u32[]{:S(2)}, u32[]{:S(2)}) %all-to-all-start) | async-done | bytes 32800 | tf_op jit(solution)/shard_map/all_to_all | solution.py:126
  43.4 3.6 %all-to-all-start.1 = ((f32[8,4,256]{2,1,0:T(4,128)}), f32[8,4,256]{2,1,0:T(4,128)S(1)}, u32[]{:S(2)}, u32[]{:S(2)}) async-start(f32[8,4,256]{2,1,0:T(4,128)} %all-to-all-done), calls=%async_computation.1 | async-start | bytes 65536 | tf_op jit(solution)/shard_map/all_to_all | solution.py:130
  47.1 0.1 iota_compare_fusion
  47.2 4.7 %all-to-all-done.1 = f32[8,4,256]{2,1,0:T(4,128)S(1)} async-done(((f32[8,4,256]{2,1,0:T(4,128)}), f32[8,4,256]{2,1,0:T(4,128)S(1)}, u32[]{:S(2)}, u32[]{:S(2)}) %all-to-all-start.1) | async-done | bytes 32800 | tf_op jit(solution)/shard_map/all_to_all | solution.py:130
  51.9 0.1 reshape.137
  52.0 0.1 fusion.10
  52.0 0.1 reshape.143
  52.1 0.1 subtract_convert_fusion.1
  52.2 0.1 maximum_bitcast_fusion
  52.3 0.1 subtract_convert_fusion
  52.4 0.2 fusion.11
  52.6 3.8 %fusion.15 = (f32[4,4,2]{2,1,0:T(4,128)S(1)}, f32[4,4,2,1024]{3,2,1,0:T(2,128)S(1)}) fusion(bf16[4,4,1024,128]{3,2,1,0:T(8,128)(2,1)} %param.12, bf16[4,4,2,64]{3,2,1,0:T(2,128)(2,1)S(1)} %bitcast.58, bf16[4,4,2,64]{3,2,1,0:T(2,128)(2,1)S(1)} %bitcast.56, pred[4,1024]{1,0:T(4,128)(4,1)S(1)} %iota_compare_fusion), kind=kOutput, calls=%fused_computation.41 | convolution fusion | flops 8536032 | bytes 4337792 | tf_op jit(solution)/shard_map/bkgd,bkld->bkgl/dot_general | solution.py:155
  56.4 0.7 fusion.4
  57.1 0.0 copy-start.8
  57.1 0.0 copy-start.5
  57.1 0.0 all-gather.11.cloned.1.call-update
  57.2 7.3 %all_gather.24 = bf16[4,4096]{1,0:T(4,128)(2,1)S(1)} all-gather(bf16[4,1024]{1,0:T(4,128)(2,1)S(1)} %convert_element_type.56), channel_id=1, replica_groups=mesh['rep'=8,'tp'=4] {'tp'}, dimensions={1}, use_global_device_ids=true | all-gather | bytes 40960 | tf_op jit(solution)/shard_map/all_gather | solution.py:183
  64.5 16.7 %all-gather.4 = bf16[8,4,4096]{2,1,0:T(4,128)(2,1)S(1)} all-gather(bf16[1,4,4096]{2,1,0:T(4,128)(2,1)S(1)} %bitcast.53), channel_id=1, replica_groups=mesh['rep'=8,'tp'=4] {'rep'}, dimensions={0}, use_global_device_ids=true | all-gather | bytes 294912 | tf_op jit(solution)/shard_map/all_gather | solution.py:184
  81.1 0.1 reshape.153
  81.2 0.5 fusion.19
  81.7 10.2 %all_to_all.48 = f32[8,4,144]{2,1,0:T(4,128)} all-to-all(f32[8,4,144]{2,1,0:T(4,128)S(1)} %reshape.139), channel_id=1, replica_groups=mesh['rep'=8,'tp'=4] {'rep'}, dimensions={0} | all-to-all | bytes 36864 | tf_op jit(solution)/shard_map/all_to_all | solution.py:126
  92.0 3.3 %all-to-all-start.6 = ((f32[8,4,144]{2,1,0:T(4,128)}), f32[8,4,144]{2,1,0:T(4,128)S(1)}, u32[]{:S(2)}, u32[]{:S(2)}) async-start(f32[8,4,144]{2,1,0:T(4,128)} %all_to_all.48), calls=%async_computation.6 | async-start | bytes 65536 | tf_op jit(solution)/shard_map/all_to_all | solution.py:130
  95.3 1.1 copy.41
  96.4 3.6 %all-to-all-done.6 = f32[8,4,144]{2,1,0:T(4,128)S(1)} async-done(((f32[8,4,144]{2,1,0:T(4,128)}), f32[8,4,144]{2,1,0:T(4,128)S(1)}, u32[]{:S(2)}, u32[]{:S(2)}) %all-to-all-start.6) | async-done | bytes 18464 | tf_op jit(solution)/shard_map/all_to_all | solution.py:130
  100.0 3.5 %all-to-all-start.4 = ((bf16[144,4,1024]{2,0,1:T(8,128)(2,1)}), bf16[144,4,1024]{2,0,1:T(8,128)(2,1)S(1)}, u32[]{:S(2)}, u32[]{:S(2)}) async-start(bf16[144,4,1024]{2,0,1:T(8,128)(2,1)} %bitcast.40), calls=%async_computation.4 | async-start | bytes 2359296 | tf_op jit(solution)/shard_map/all_to_all | solution.py:120
  103.5 0.0 all-gather.9.cloned.1.call-start
  103.6 0.6 dynamic-slice
  104.8 0.1 multiply_reduce_fusion
  104.9 0.2 dynamic-update-slice
  105.2 16.0 %all-reduce = f32[16]{0:T(128)S(1)} all-reduce(f32[16]{0:T(128)S(1)} %dynamic-update-slice), channel_id=4, replica_groups=mesh['rep'=8,'tp'=4] {'tp'}, use_global_device_ids=true, to_apply=%add | all-reduce | flops 16 | bytes 128
  121.1 0.1 reshape.141
  121.2 0.1 reshape.146
  121.4 0.7 multiply_multiply_fusion
  122.0 0.0 all-to-all-done.4
  122.0 1.1 copy-done.2
  123.1 0.0 all-gather.9.cloned.1.call-update
  123.1 0.0 all-gather.13.cloned.1.call-done
  123.2 5.0 %all-to-all-start.3 = ((bf16[4,128,4608]{2,1,0:T(8,128)(2,1)}), bf16[4,128,4608]{2,1,0:T(8,128)(2,1)}, u32[]{:S(2)}, u32[]{:S(2)}) async-start(bf16[4,128,4608]{2,1,0:T(8,128)(2,1)} %bitcast.43), calls=%async_computation.3 | async-start | bytes 9437184 | tf_op jit(solution)/shard_map/all_to_all | solution.py:116
  128.1 67.3 %all-gather.11.cloned.1.call-done = bf16[512,4608]{1,0:T(8,128)(2,1)} async-done(((bf16[128,4608]{1,0:T(8,128)(2,1)}), bf16[512,4608]{1,0:T(8,128)(2,1)}) %all-gather.11.cloned.1.call-update) | async-done | bytes 4718608 | tf_op jit(solution)/shard_map/all_gather | solution.py:115
  195.5 0.0 all-to-all-done.3.refs_1_
  195.5 4.9 %all-to-all-start.2 = ((bf16[4,128,4608]{2,1,0:T(8,128)(2,1)}), bf16[4,128,4608]{2,1,0:T(8,128)(2,1)}, u32[]{:S(2)}, u32[]{:S(2)}) async-start(bf16[4,128,4608]{2,1,0:T(8,128)(2,1)} %bitcast.44), calls=%async_computation.2 | async-start | bytes 9437184 | tf_op jit(solution)/shard_map/all_to_all | solution.py:116
  200.4 0.1 collective-permute-start.1
  200.5 53.2 %all-to-all-done.2.refs_0_ = bf16[4,128,4608]{2,1,0:T(8,128)(2,1)} async-done(((bf16[4,128,4608]{2,1,0:T(8,128)(2,1)}), bf16[4,128,4608]{2,1,0:T(8,128)(2,1)}, u32[]{:S(2)}, u32[]{:S(2)}) %all-to-all-start.2) | async-done | bytes 4718624 | tf_op jit(solution)/shard_map/all_to_all | solution.py:116
  253.7 0.0 collective-permute-start
  253.7 0.0 collective-permute-done.1.refs_3_
  253.7 8.9 %collective-permute-done.refs_2_ = bf16[4,128,4608]{2,1,0:T(8,128)(2,1)} collective-permute-done((bf16[4,128,4608]{2,1,0:T(8,128)(2,1)}, bf16[4,128,4608]{2,1,0:T(8,128)(2,1)}, u32[]{:S(2)}, u32[]{:S(2)}) %collective-permute-start) | collective-permute-done | bytes 4718624 | tf_op jit(solution)/shard_map/ppermute | solution.py:181
  262.5 21.4 %join.1 = bf16[4608,2048]{1,0:T(8,128)(2,1)} custom-call(bf16[4,128,4608]{2,1,0:T(8,128)(2,1)} %all-to-all-done.2.refs_0_, bf16[4,128,4608]{2,1,0:T(8,128)(2,1)} %all-to-all-done.3.refs_1_, bf16[4,128,4608]{2,1,0:T(8,128)(2,1)} %collective-permute-done.refs_2_, bf16[4,128,4608]{2,1,0:T(8,128)(2,1)} %collective-permute-done.1.refs_3_), custom_call_target="tpu_custom_call" | custom-call | bytes 37748736 | tf_op jit(solution)/shard_map/join/pallas_call | solution.py:64
  284.0 2.3 all-gather.9.cloned.1.call-done
  286.3 12.5 %turn.1 = bf16[1024,4608]{1,0:T(8,128)(2,1)} custom-call(bf16[4608,1024]{1,0:T(8,128)(2,1)} %bitcast.42), custom_call_target="tpu_custom_call" | custom-call | bytes 18874368 | tf_op jit(solution)/shard_map/turn/pallas_call | solution.py:82
  (30 shorter events, 0.2 us)
Async XLA Ops:
  7.2 21.0 %copy-start.3 = (bf16[64,4608]{1,0:T(8,128)(2,1)S(1)}, bf16[64,4608]{1,0:T(8,128)(2,1)}, u32[]{:S(2)}) copy-start(bf16[64,4608]{1,0:T(8,128)(2,1)} %param.16) | copy-start | bytes 1769476
  7.2 21.2 %copy-start.4 = (bf16[64,4608]{1,0:T(8,128)(2,1)S(1)}, bf16[64,4608]{1,0:T(8,128)(2,1)}, u32[]{:S(2)}) copy-start(bf16[64,4608]{1,0:T(8,128)(2,1)} %param.17) | copy-start | bytes 1769476
  7.2 21.5 %copy-start.1 = (bf16[128,4608]{1,0:T(8,128)(2,1)S(1)}, bf16[128,4608]{1,0:T(8,128)(2,1)}, u32[]{:S(2)}) copy-start(bf16[128,4608]{1,0:T(8,128)(2,1)} %param.15) | copy-start | bytes 3538948
  7.2 27.9 %copy-start.6 = (s32[4]{0:T(128)S(1)}, s32[4]{0:T(128)}, u32[]{:S(2)}) copy-start(s32[4]{0:T(128)} %param.11) | copy-start | bytes 52
  7.2 116.0 %all-gather.13.cloned.1.call-start = ((), (), s32[]{:S(2)}) async-start(), calls=%async_computation.9 | async-start | bytes 5898240 | tf_op jit(solution)/shard_map/all_gather | solution.py:115
  29.9 13.5 %all-to-all-start = ((f32[8,4,256]{2,1,0:T(4,128)}), f32[8,4,256]{2,1,0:T(4,128)}, u32[]{:S(2)}, u32[]{:S(2)}) async-start(f32[8,4,256]{2,1,0:T(4,128)} %reshape.134), calls=%async_computation | async-start | bytes 65536 | tf_op jit(solution)/shard_map/all_to_all | solution.py:126
  43.4 8.4 %all-to-all-start.1 = ((f32[8,4,256]{2,1,0:T(4,128)}), f32[8,4,256]{2,1,0:T(4,128)S(1)}, u32[]{:S(2)}, u32[]{:S(2)}) async-start(f32[8,4,256]{2,1,0:T(4,128)} %all-to-all-done), calls=%async_computation.1 | async-start | bytes 65536 | tf_op jit(solution)/shard_map/all_to_all | solution.py:130
  47.1 148.4 %all-gather.11.cloned.1.call-start = ((), (), s32[]{:S(2)}) async-start(), calls=%async_computation.8 | async-start | bytes 5898240 | tf_op jit(solution)/shard_map/all_gather | solution.py:115
  52.1 4.2 %copy-start.7 = (bf16[4,4,1024,128]{3,2,1,0:T(8,128)(2,1)S(1)}, bf16[4,4,1024,128]{3,2,1,0:T(8,128)(2,1)}, u32[]{:S(2)}) copy-start(bf16[4,4,1024,128]{3,2,1,0:T(8,128)(2,1)} %param.13) | copy-start | bytes 12582916
  56.3 24.9 %copy-start = (bf16[144,4096]{1,0:T(8,128)(2,1)S(1)}, bf16[144,4096]{1,0:T(8,128)(2,1)}, u32[]{:S(2)}) copy-start(bf16[144,4096]{1,0:T(8,128)(2,1)} %param.18) | copy-start | bytes 3538948
  57.1 46.5 %copy-start.8 = (u32[32]{0:T(128)S(1)}, u32[32]{0:T(128)}, u32[]{:S(2)}) copy-start(u32[32]{0:T(128)} %constant.34) | copy-start | bytes 388
  57.1 64.2 %copy-start.5 = (f32[1152]{0:T(1024)S(1)}, f32[1152]{0:T(1024)}, u32[]{:S(2)}) copy-start(f32[1152]{0:T(1024)} %param.19) | copy-start | bytes 13828
  92.0 8.0 %all-to-all-start.6 = ((f32[8,4,144]{2,1,0:T(4,128)}), f32[8,4,144]{2,1,0:T(4,128)S(1)}, u32[]{:S(2)}, u32[]{:S(2)}) async-start(f32[8,4,144]{2,1,0:T(4,128)} %all_to_all.48), calls=%async_computation.6 | async-start | bytes 65536 | tf_op jit(solution)/shard_map/all_to_all | solution.py:130
  100.0 22.1 %all-to-all-start.4 = ((bf16[144,4,1024]{2,0,1:T(8,128)(2,1)}), bf16[144,4,1024]{2,0,1:T(8,128)(2,1)S(1)}, u32[]{:S(2)}, u32[]{:S(2)}) async-start(bf16[144,4,1024]{2,0,1:T(8,128)(2,1)} %bitcast.40), calls=%async_computation.4 | async-start | bytes 2359296 | tf_op jit(solution)/shard_map/all_to_all | solution.py:120
  103.5 182.8 %all-gather.9.cloned.1.call-start = ((), (), s32[]{:S(2)}) async-start(), calls=%async_computation.7 | async-start | bytes 10616832 | tf_op jit(solution)/shard_map/all_gather | solution.py:195
  122.0 1.1 copy-start.2
  123.2 72.3 %all-to-all-start.3 = ((bf16[4,128,4608]{2,1,0:T(8,128)(2,1)}), bf16[4,128,4608]{2,1,0:T(8,128)(2,1)}, u32[]{:S(2)}, u32[]{:S(2)}) async-start(bf16[4,128,4608]{2,1,0:T(8,128)(2,1)} %bitcast.43), calls=%async_computation.3 | async-start | bytes 9437184 | tf_op jit(solution)/shard_map/all_to_all | solution.py:116
  195.5 58.2 %all-to-all-start.2 = ((bf16[4,128,4608]{2,1,0:T(8,128)(2,1)}), bf16[4,128,4608]{2,1,0:T(8,128)(2,1)}, u32[]{:S(2)}, u32[]{:S(2)}) async-start(bf16[4,128,4608]{2,1,0:T(8,128)(2,1)} %bitcast.44), calls=%async_computation.2 | async-start | bytes 9437184 | tf_op jit(solution)/shard_map/all_to_all | solution.py:116
  200.4 53.2 %collective-permute-start.1 = (bf16[4,128,4608]{2,1,0:T(8,128)(2,1)}, bf16[4,128,4608]{2,1,0:T(8,128)(2,1)}, u32[]{:S(2)}, u32[]{:S(2)}) collective-permute-start(bf16[4,128,4608]{2,1,0:T(8,128)(2,1)} %all-to-all-done.3.refs_1_), channel_id=1, source_target_pairs={{4,0},{0,4},{12,8},{8,12},{20,16},{16,20},{28,24},{24,28},{5,1},{1... | collective-permute-start | bytes 14155784 | tf_op jit(solution)/shard_map/ppermute | solution.py:181
  253.7 8.9 %collective-permute-start = (bf16[4,128,4608]{2,1,0:T(8,128)(2,1)}, bf16[4,128,4608]{2,1,0:T(8,128)(2,1)}, u32[]{:S(2)}, u32[]{:S(2)}) collective-permute-start(bf16[4,128,4608]{2,1,0:T(8,128)(2,1)} %all-to-all-done.2.refs_0_), channel_id=1, source_target_pairs={{4,0},{0,4},{12,8},{8,12},{20,16},{16,20},{28,24},{24,28},{5,1},{1... | collective-permute-start | bytes 14155784 | tf_op jit(solution)/shard_map/ppermute | solution.py:181
Sparse Core Ops, SparseCore 0:
  10.2 95.8 all-gather.12
  107.6 87.8 all-gather.10
  197.1 89.1 all-gather.8
where the time goes:
time: 307 us; the launch traced here: 305 us
  waiting for transfers between devices  148 us (48%)
  blocking collectives  66.7 us (22%)
  Pallas kernels  34 us (11%)
  starting transfers between devices  25.7 us (8%)
  between operations  14.6 us (5%)
  matrix products  6.16 us (2%)
  other arithmetic  5.75 us (2%)
  local copies, waits for them, and re-layouts  4.25 us (1%)
    all_gather x2, waiting for transfers between devices, collect(): lax.all_gather(rows[None], 'rep', axis=0, tiled=True, axis_index_groups=g...  67.4 us
    all_to_all x2, waiting for transfers between devices, collect(): return lax.all_to_all(planes, 'tp', split_axis=0, concat_axis=0, tiled=True)  53.2 us
    pallas_call x1, Pallas kernels, join(): pl.pallas_call(functools.partial(join_kernel, per_tp, q_rows, k_rows), gr...  21.4 us
    all_gather x1, blocking collectives, body(): attention_all = lax.all_gather(own_all, 'rep', axis=0, tiled=True)  16.7 us
    all_gather x1, blocking collectives, body(): normed_all = lax.all_gather(normed, 'rep', axis=0, tiled=True)  16.5 us
    unnamed x1, blocking collectives  16 us
    pallas_call x1, Pallas kernels, turn(): pl.pallas_call(turn_kernel, grid=(height // stripe,), in_specs=[pl.BlockS...  12.5 us
    all_to_all x1, blocking collectives, scatter_rows(): lax.all_to_all(wide, 'rep', split_axis=0, concat_axis=0, tiled=True)  10.2 us
  transfers between devices with their start and end apart: 11, of which 7 were waited for; matrix products, arithmetic and copies ran while one was open for 4% of the time, Pallas kernels for 7%

commit v1 on v0

--- a/solution.py
+++ b/solution.py
@@ -2,11 +2,13 @@
 
 import jax
 import jax.numpy as jnp
+import numpy as np
 from jax import lax
 from jax.experimental import pallas as pl
 from jax.experimental.pallas import tpu as pltpu
 from jax.sharding import PartitionSpec as P
 
+MESH = pl.DeviceIdType.MESH
 score_scale = 144.0 ** (-0.5)
 soft_cap = 50.0
 
@@ -92,7 +94,7 @@
     )(rows)
 
 
-def body(
+def general_body(
     hidden, positions, key_cache, value_cache, norm_gain, q_proj, k_proj, v_proj, o_proj, post_gain
 ):
     tp_count = lax.axis_size("tp")
@@ -197,18 +199,530 @@
     return (joined_block, out_block, result.astype(jnp.bfloat16))
 
 
+def move_kernel(
+    sizes,
+    q_ref, k_ref, v_ref, o_ref,
+    hidden_ref, positions_ref, keys_ref, values_ref, gain_ref, post_ref, freq_ref,
+    joined, heads, result,
+    stage, q_own, kv_own, o_rows,
+    hidden, positions, keys, values, gain, post, freq,
+    fresh, q_heads, k_heads, v_heads, attended, partial, others, squares, squares_in,
+    early_sems, share_send, share_recv, square_send, square_recv,
+    local_sems, kv_sems, rows_send, rows_recv,
+    line_send, line_recv, plane_send, plane_recv,
+    twin_send, twin_recv, twin_wo_send, twin_wo_recv,
+):
+    planes, cores, cols, pieces = sizes
+    rep, t = lax.axis_index("rep"), lax.axis_index("tp")
+    z, c = rep // cores, lax.rem(rep, cores)
+    other = 1 - c
+    width = q_ref.shape[1]
+    deep = width // pieces
+    q_rows, k_rows = q_ref.shape[0], k_ref.shape[0]
+    o_own = o_ref.shape[0]
+    block = cols * cores * o_own
+    half = heads.shape[0] // cores
+    wo_rows = half // pieces
+    moving = 2 * pieces
+    total = 3 * pieces
+    q_all = cores * cols * q_rows
+    k_all = cores * cols * k_rows
+    even = lax.rem(t, 2) == 0
+
+    def at(zz, cc, tt):
+        return (zz * cores + cc, tt)
+
+    def column(tt, j, cc):
+        parity = lax.rem(tt, 2)
+        q_at = (cc * cols + tt) * q_rows
+        kv_at = q_all + parity * k_all + (cc * cols + tt - parity) * k_rows
+        is_q = (j < pieces).astype(jnp.int32)
+        return pl.multiple_of(is_q * q_at + (1 - is_q) * kv_at, 128)
+
+    def slot(tt, j, cc):
+        row = pl.multiple_of(lax.rem(j, pieces) * deep, 128)
+        return joined.at[pl.ds(row, deep), pl.ds(column(tt, j, cc), 128)]
+
+    def wo_slot(zz, j, cc):
+        row = pl.multiple_of(cc * half + (j - moving) * wo_rows, 128)
+        col = pl.multiple_of(zz * block, 128)
+        return heads.at[pl.ds(row, wo_rows), pl.ds(col, block)]
+
+    def remote(src, dst, send, recv, device):
+        return pltpu.make_async_remote_copy(
+            src_ref=src, dst_ref=dst, send_sem=send, recv_sem=recv,
+            device_id=device, device_id_type=MESH,
+        )
+
+    def line_copy(zz, j, way, device):
+        return remote(stage.at[zz, j], stage.at[zz, j], line_send.at[way, zz, j],
+                      line_recv.at[zz, j], device)
+
+    def line_wo_copy(zz, j, way, device):
+        return remote(wo_slot(zz, j, c), wo_slot(zz, j, c), line_send.at[way, zz, j],
+                      line_recv.at[zz, j], device)
+
+    def plane_copy(zz, j):
+        return remote(stage.at[zz, j], slot(t, j, c), plane_send.at[zz, j],
+                      plane_recv.at[t, j], at(z, c, zz))
+
+    def plane_arrival(tt, j):
+        return remote(slot(tt, j, c), slot(tt, j, c), plane_send.at[0, j],
+                      plane_recv.at[tt, j], at(z, c, tt))
+
+    def twin_copy(src, tt, j, cc):
+        return remote(src, slot(tt, j, cc), twin_send.at[tt, j], twin_recv.at[tt, j], at(z, other, t))
+
+    def twin_wo_copy(zz, j, cc):
+        return remote(wo_slot(zz, j, cc), wo_slot(zz, j, cc), twin_wo_send.at[zz, j - moving],
+                      twin_wo_recv.at[zz, j - moving], at(z, other, t))
+
+    def rows_copy(dc, dt):
+        cc, tt = lax.rem(c + dc, cores), lax.rem(t + dt, cols)
+        mine = c * cols + t
+        src_at = pl.multiple_of((tt * cores + cc) * half, 128)
+        dst_at = pl.multiple_of(mine * o_own, 16)
+        return remote(o_ref.at[:, pl.ds(src_at, half)], o_rows.at[pl.ds(dst_at, o_own), :],
+                      rows_send.at[dc * cols + dt], rows_recv.at[mine], at(z, cc, tt))
+
+    def rows_arrival(dc, dt):
+        cc, tt = lax.rem(c + dc, cores), lax.rem(t + dt, cols)
+        theirs = cc * cols + tt
+        dst_at = pl.multiple_of(theirs * o_own, 16)
+        view = o_rows.at[pl.ds(dst_at, o_own), :]
+        return remote(view, view, rows_send.at[dc * cols + dt], rows_recv.at[theirs], at(z, cc, tt))
+
+    peers = [(dc, dt) for dc in range(cores) for dt in range(cols) if dc or dt]
+
+    barrier = pltpu.get_barrier_semaphore()
+    for dc, dt in peers:
+        pl.semaphore_signal(
+            barrier, inc=1, device_id=at(z, lax.rem(c + dc, cores), lax.rem(t + dt, cols)),
+            device_id_type=MESH)
+
+    @pl.when(z > 0)
+    def _():
+        pl.semaphore_signal(barrier, inc=1, device_id=at(z - 1, c, t), device_id_type=MESH)
+
+    @pl.when(z < planes - 1)
+    def _():
+        pl.semaphore_signal(barrier, inc=1, device_id=at(z + 1, c, t), device_id_type=MESH)
+
+    load_q = pltpu.make_async_copy(q_ref, q_own, local_sems.at[0])
+    load_q.start()
+    mine = c * cols + t
+    load_o = pltpu.make_async_copy(
+        o_ref.at[:, pl.ds(pl.multiple_of((t * cores + c) * half, 128), half)],
+        o_rows.at[pl.ds(pl.multiple_of(mine * o_own, 16), o_own), :], local_sems.at[1])
+    load_o.start()
+    load_k = pltpu.make_async_copy(k_ref, kv_own.at[pl.ds(0, k_rows)], local_sems.at[2])
+    load_v = pltpu.make_async_copy(v_ref, kv_own.at[pl.ds(k_rows, k_rows)], local_sems.at[2])
+
+    @pl.when(even)
+    def _():
+        load_k.start()
+
+    @pl.when(jnp.logical_not(even))
+    def _():
+        load_v.start()
+
+    give_v = remote(v_ref, kv_own.at[pl.ds(0, k_rows)], kv_sems.at[0], kv_sems.at[1], at(z, c, t + 1 - 2 * lax.rem(t, 2)))
+    give_k = remote(k_ref, kv_own.at[pl.ds(k_rows, k_rows)], kv_sems.at[0], kv_sems.at[1], at(z, c, t + 1 - 2 * lax.rem(t, 2)))
+
+    early = [
+        pltpu.make_async_copy(source, target, early_sems.at[i])
+        for i, (source, target) in enumerate((
+            (hidden_ref, hidden), (positions_ref, positions), (gain_ref, gain), (post_ref, post),
+            (freq_ref, freq), (keys_ref, keys), (values_ref, values)))
+    ]
+
+    batch, kv_local, length, head_dim = keys_ref.shape
+    q_local = q_all // head_dim
+    group = q_local // kv_local
+    f32, bf16 = jnp.float32, jnp.bfloat16
+
+    def project():
+        for copy in early[:5]:
+            copy.wait()
+        wide = hidden[...].astype(f32)
+        mean_square = jnp.mean(wide * wide, axis=-1, keepdims=True)
+        normed = (wide * lax.rsqrt(mean_square + 1e-06) * gain[...]).astype(bf16)
+
+        def columns(i, carry):
+            span = pl.ds(pl.multiple_of(i * 256, 256), 256)
+            fresh[:, span] = jnp.dot(normed, joined[:, span], preferred_element_type=f32)
+            return carry
+
+        lax.fori_loop(0, fresh.shape[1] // 256, columns, 0)
+        angle = jnp.concatenate(
+            [positions[b].astype(f32) * freq[...] for b in range(batch)], axis=0)
+        cosine, sine = jnp.cos(angle), jnp.sin(angle)
+        lane = lax.broadcasted_iota(jnp.int32, angle.shape, 1)
+        sine = jnp.where(lane < head_dim // 2, -sine, sine)
+
+        def turned(start):
+            x = fresh[:, start : start + head_dim]
+            swapped = pltpu.roll(x, head_dim // 2, 1)
+            return (x * cosine + swapped * sine).astype(bf16).astype(f32)
+
+        for h in range(kv_local):
+            key = turned(q_all + h * head_dim)
+            at_v = q_all + k_all + h * head_dim
+            value = fresh[:, at_v : at_v + head_dim].astype(bf16).astype(f32)
+            for g in range(group):
+                n = h * group + g
+                query = turned(n * head_dim)
+                for b in range(batch):
+                    q_heads[b, n : n + 1, :] = query[b : b + 1]
+                    k_heads[b, n : n + 1, :] = key[b : b + 1]
+                    v_heads[b, n : n + 1, :] = value[b : b + 1]
+
+    def attend():
+        for copy in early[5:]:
+            copy.wait()
+        over = (((1,), (1,)), ((), ()))
+        slots = lax.broadcasted_iota(jnp.int32, (q_local, length), 1)
+        owner = lax.broadcasted_iota(jnp.int32, (q_local, 1), 0) // group
+        for b in range(batch):
+            query = q_heads[b]
+            narrow = query.astype(bf16)
+            scores = jnp.zeros((q_local, length), f32)
+            for h in range(kv_local):
+                one = lax.dot_general(narrow, keys[b, h], over, preferred_element_type=f32)
+                scores = jnp.where(owner == h, one, scores)
+            raw = jnp.exp(soft_cap * jnp.tanh(scores * score_scale / soft_cap))
+            raw = jnp.where(slots < positions[b], raw, 0.0)
+            self_score = jnp.sum(query * k_heads[b], axis=-1, keepdims=True) * score_scale
+            self_raw = jnp.exp(soft_cap * jnp.tanh(self_score / soft_cap))
+            denom = jnp.sum(raw, axis=-1, keepdims=True) + self_raw
+            weights = (raw / denom).astype(bf16)
+            self_weight = (self_raw / denom).astype(bf16).astype(f32)
+            mixed = jnp.zeros((q_local, head_dim), f32)
+            for h in range(kv_local):
+                one = jnp.dot(weights, values[b, h], preferred_element_type=f32)
+                mixed = jnp.where(owner == h, one, mixed)
+            mixed = mixed + self_weight * v_heads[b]
+            for n in range(q_local):
+                attended[b : b + 1, n * head_dim : (n + 1) * head_dim] = mixed[n : n + 1]
+
+    def share_copy(p, device):
+        return remote(partial.at[p], others.at[t], share_send.at[p], share_recv.at[t], device)
+
+    def square_copy(p):
+        return remote(squares, squares_in.at[t], square_send.at[p], square_recv.at[t], at(z, c, p))
+
+    def finish():
+        narrow = attended[...].astype(bf16)
+
+        def slices(p, carry):
+            span = pl.ds(pl.multiple_of(p * block, 128), block)
+            partial[p] = jnp.dot(narrow, heads[:, span], preferred_element_type=f32)
+            return carry
+
+        lax.fori_loop(0, cols, slices, 0)
+        for dt in range(1, cols):
+            p = lax.rem(t + dt, cols)
+            share_copy(p, at(z, c, p)).start()
+        share = partial[t]
+        for dt in range(1, cols):
+            p = lax.rem(t + dt, cols)
+            remote(others.at[p], others.at[p], share_send.at[p], share_recv.at[p], at(z, c, p)).wait_recv()
+            share = share + others[p]
+        square = jnp.sum(share * share, axis=-1, keepdims=True)
+        squares[...] = jnp.broadcast_to(square, squares.shape)
+        for dt in range(1, cols):
+            square_copy(lax.rem(t + dt, cols)).start()
+        total_square = square
+        for dt in range(1, cols):
+            p = lax.rem(t + dt, cols)
+            remote(squares_in.at[p], squares_in.at[p], square_send.at[p], square_recv.at[p],
+                   at(z, c, p)).wait_recv()
+            total_square = total_square + squares_in[p][:, :1]
+        multiplier = lax.rsqrt(total_square / width + 1e-06)
+        result[...] = (share * multiplier * post[...]).astype(result.dtype)
+        for dt in range(1, cols):
+            p = lax.rem(t + dt, cols)
+            share_copy(p, at(z, c, p)).wait_send()
+            square_copy(p).wait_send()
+
+    def prepare(j):
+        @pl.when(j < pieces)
+        def _():
+            span = pl.ds(pl.multiple_of(j * deep, 128), deep)
+            stage[z, j] = jnp.transpose(q_own[:, span])
+
+        @pl.when(j == pieces)
+        def _():
+            @pl.when(even)
+            def _():
+                load_k.wait()
+                give_k.wait_recv()
+
+            @pl.when(jnp.logical_not(even))
+            def _():
+                load_v.wait()
+                give_v.wait_recv()
+
+        @pl.when(jnp.logical_and(j >= pieces, j < moving))
+        def _():
+            span = pl.ds(pl.multiple_of((j - pieces) * deep, 128), deep)
+            stage[z, j] = jnp.transpose(kv_own[:, span])
+
+        @pl.when(j == moving)
+        def _():
+            load_o.wait()
+            for dc, dt in peers:
+                rows_arrival(dc, dt).wait_recv()
+
+        @pl.when(jnp.logical_and(j >= moving, j < total))
+        def _():
+            col = pl.multiple_of((j - moving) * wo_rows, 128)
+            row = pl.multiple_of(c * half + (j - moving) * wo_rows, 128)
+            heads[pl.ds(row, wo_rows), pl.ds(pl.multiple_of(z * block, 128), block)] = jnp.transpose(
+                o_rows[:, pl.ds(col, wo_rows)])
+
+    def send_line(zz, j, way):
+        target = at(z - 1, c, t) if way == 0 else at(z + 1, c, t)
+        room = z > 0 if way == 0 else z < planes - 1
+
+        @pl.when(jnp.logical_and(room, j < moving))
+        def _():
+            line_copy(zz, j, way, target).start()
+
+        @pl.when(jnp.logical_and(room, j >= moving))
+        def _():
+            line_wo_copy(zz, j, way, target).start()
+
+    def wait_line(zz, j):
+        @pl.when(j < moving)
+        def _():
+            line_copy(zz, j, 0, at(z, other, t)).wait_recv()
+
+        @pl.when(j >= moving)
+        def _():
+            line_wo_copy(zz, j, 0, at(z, other, t)).wait_recv()
+
+    def deliver(zz, j):
+        @pl.when(jnp.logical_and(j < moving, t != zz))
+        def _():
+            plane_copy(zz, j).start()
+
+        @pl.when(jnp.logical_and(j < moving, t == zz))
+        def _():
+            row = pl.multiple_of(lax.rem(j, pieces) * deep, 128)
+            joined[pl.ds(row, deep), pl.ds(column(t, j, c), 128)] = stage[zz, j]
+            twin_copy(stage.at[zz, j], t, j, c).start()
+
+        @pl.when(j >= moving)
+        def _():
+            twin_wo_copy(zz, j, c).start()
+
+    for copy in early[:5]:
+        copy.start()
+    load_q.wait()
+    prepare(jnp.int32(0))
+    prepare(jnp.int32(1))
+    n_line = (z > 0).astype(jnp.int32) + (z < planes - 1).astype(jnp.int32)
+    pl.semaphore_wait(barrier, len(peers) + n_line)
+
+    def rounds(r, carry):
+        @pl.when(r < total)
+        def _():
+            send_line(z, r, 0)
+            send_line(z, r, 1)
+            deliver(z, r)
+
+        @pl.when(r == 0)
+        def _():
+            @pl.when(even)
+            def _():
+                give_v.start()
+
+            @pl.when(jnp.logical_not(even))
+            def _():
+                give_k.start()
+
+        @pl.when(r == 1)
+        def _():
+            for dc, dt in peers:
+                rows_copy(dc, dt).start()
+            for copy in early[5:]:
+                copy.start()
+
+        @pl.when(r + 2 < total)
+        def _():
+            prepare(r + 2)
+
+        for k in range(1, planes):
+            for way in (0, 1):
+                zz = z + k if way == 0 else z - k
+                j = r - k
+                inside = zz < planes if way == 0 else zz >= 0
+
+                @pl.when(jnp.logical_and(inside, jnp.logical_and(j >= 0, j < total)))
+                def _():
+                    wait_line(zz, j)
+                    send_line(zz, j, way)
+                    deliver(zz, j)
+
+        far = jnp.where(z > t, z - t, t - z)
+        j = r - far - 1
+
+        @pl.when(jnp.logical_and(j >= 0, j < moving))
+        def _():
+            for dt in range(1, cols):
+                tt = lax.rem(t + dt, cols)
+                plane_arrival(tt, j).wait_recv()
+                twin_copy(slot(tt, j, c), tt, j, c).start()
+
+        @pl.when(r == moving + 1 + far)
+        def _():
+            lax.fori_loop(0, moving, twin_in, 0)
+            project()
+
+        @pl.when(r == moving + 2 + far)
+        def _():
+            attend()
+        return carry
+
+    def twin_in(j, carry):
+        for tt in range(cols):
+            twin_copy(slot(tt, j, other), tt, j, other).wait_recv()
+        return carry
+
+    lax.fori_loop(0, total + planes - 1, rounds, 0)
+
+    def twin_wo_in(j, carry):
+        for zz in range(planes):
+            twin_wo_copy(zz, j, other).wait_recv()
+        return carry
+
+    lax.fori_loop(moving, total, twin_wo_in, 0)
+    finish()
+
+    def sent(j, carry):
+        for zz in range(planes):
+            for way in (0, 1):
+                room = z > 0 if way == 0 else z < planes - 1
+                passes = z <= zz if way == 0 else z >= zz
+
+                @pl.when(jnp.logical_and(room, passes))
+                def _():
+                    @pl.when(j < moving)
+                    def _():
+                        line_copy(zz, j, way, at(z, other, t)).wait_send()
+
+                    @pl.when(j >= moving)
+                    def _():
+                        line_wo_copy(zz, j, way, at(z, other, t)).wait_send()
+
+            @pl.when(jnp.logical_and(j < moving, t != zz))
+            def _():
+                plane_copy(zz, j).wait_send()
+
+            @pl.when(j < moving)
+            def _():
+                twin_copy(slot(zz, j, c), zz, j, c).wait_send()
+
+            @pl.when(j >= moving)
+            def _():
+                twin_wo_copy(zz, j, c).wait_send()
+        return carry
+
+    lax.fori_loop(0, total, sent, 0)
+    for dc, dt in peers:
+        rows_copy(dc, dt).wait_send()
+
+    @pl.when(even)
+    def _():
+        give_v.wait_send()
+
+    @pl.when(jnp.logical_not(even))
+    def _():
+        give_k.wait_send()
+
+
+def line_body(hidden, positions, key_cache, value_cache, norm_gain, q_proj, k_proj, v_proj, o_proj, post_gain):
+    cols = lax.axis_size("tp")
+    cores = 2
+    planes = lax.axis_size("rep") // cores
+    pieces = 4
+    width = q_proj.shape[1]
+    deep = width // pieces
+    q_rows, k_rows, o_own = q_proj.shape[0], k_proj.shape[0], o_proj.shape[0]
+    features = o_proj.shape[1] // cols
+    columns = cores * cols * (q_rows + 2 * k_rows)
+    model = o_own * cores * cols * planes
+    bf = jnp.bfloat16
+    dma = pltpu.SemaphoreType.DMA
+    hbm = pl.BlockSpec(memory_space=pltpu.HBM)
+    f32 = jnp.float32
+    batch, kv_local, length, head_dim = key_cache.shape
+    q_local = cores * cols * q_rows // head_dim
+    half = head_dim // 2
+    freq = 10000.0 ** (-2.0 * np.arange(half) / head_dim)
+    freq = jnp.asarray(np.concatenate([freq, freq])[None], f32)
+    share = post_gain.shape[0]
+    moving, total = 2 * pieces, 3 * pieces
+    out = pl.pallas_call(
+        functools.partial(move_kernel, (planes, cores, cols, pieces)),
+        in_specs=[hbm] * 11,
+        out_shape=[
+            pltpu.VMEM((width, columns), bf),
+            pltpu.VMEM((features, model), bf),
+            jax.ShapeDtypeStruct((hidden.shape[0], post_gain.shape[0]), bf),
+        ],
+        out_specs=[pl.BlockSpec(memory_space=pltpu.VMEM)] * 3,
+        scratch_shapes=[
+            pltpu.VMEM((planes, moving, deep, 128), bf),
+            pltpu.VMEM((q_rows, width), bf),
+            pltpu.VMEM((2 * k_rows, width), bf),
+            pltpu.VMEM((cores * cols * o_own, features // cores), bf),
+            pltpu.VMEM(hidden.shape, bf), pltpu.SMEM(positions.shape, jnp.int32),
+            pltpu.VMEM(key_cache.shape, bf), pltpu.VMEM(value_cache.shape, bf),
+            pltpu.VMEM((1, width), f32), pltpu.VMEM((1, share), f32), pltpu.VMEM((1, head_dim), f32),
+            pltpu.VMEM((batch, columns), f32), pltpu.VMEM((batch, q_local, head_dim), f32),
+            pltpu.VMEM((batch, q_local, head_dim), f32), pltpu.VMEM((batch, q_local, head_dim), f32),
+            pltpu.VMEM((batch, features), f32), pltpu.VMEM((cols, batch, share), f32),
+            pltpu.VMEM((cols, batch, share), f32), pltpu.VMEM((batch, 128), f32),
+            pltpu.VMEM((cols, batch, 128), f32),
+            dma((7,)), dma((cols,)), dma((cols,)), dma((cols,)), dma((cols,)),
+            dma((3,)), dma((2,)), dma((cores * cols,)), dma((cores * cols,)),
+            dma((2, planes, total)), dma((planes, total)), dma((planes, moving)), dma((cols, moving)),
+            dma((cols, moving)), dma((cols, moving)), dma((planes, pieces)), dma((planes, pieces)),
+        ],
+        compiler_params=pltpu.CompilerParams(
+            collective_id=0, has_side_effects=True, vmem_limit_bytes=VLIM),
+        name="move",
+    )(q_proj, k_proj, v_proj, o_proj, hidden, positions, key_cache, value_cache,
+      norm_gain[None], post_gain[None], freq)
+    return tuple(out)
+
+VLIM = 34 * 2**20
+
+
+def body(*args):
+    cols, reps = lax.axis_size("tp"), lax.axis_size("rep")
+    key_cache, q_proj, k_proj, o_proj = args[2], args[5], args[6], args[8]
+    lanes = 128
+    fits = (
+        reps == 2 * cols
+        and cols % 2 == 0
+        and key_cache.shape[3] == lanes
+        and q_proj.shape[0] == lanes
+        and 2 * k_proj.shape[0] == lanes
+        and o_proj.shape[0] % 16 == 0
+        and q_proj.shape[1] % (4 * lanes) == 0
+        and o_proj.shape[1] % (8 * lanes * cols) == 0
+        and (2 * cols * o_proj.shape[0]) % lanes == 0
+    )
+    return (line_body if fits else general_body)(*args)
+
+
 def solution(mesh):
     in_specs = (
-        P("rep", None),
-        P("rep"),
-        P("rep", "tp", None, None),
-        P("rep", "tp", None, None),
-        P(),
-        P(("rep", "tp"), None),
-        P(("rep", "tp"), None),
-        P(("rep", "tp"), None),
-        P(("rep", "tp"), None),
-        P("tp"),
+        P("rep", None), P("rep"), P("rep", "tp", None, None), P("rep", "tp", None, None), P(),
+        P(("rep", "tp"), None), P(("rep", "tp"), None), P(("rep", "tp"), None), P(("rep", "tp"), None), P("tp"),
     )
     out_specs = (P(None, "tp"), P("tp", None), P("rep", "tp"))
     return jax.shard_map(body, mesh=mesh, in_specs=in_specs, out_specs=out_specs, check_vma=False)

time: 307 us -> 263 us (0.86)
  Pallas kernels: 34 us -> 248 us
  waiting for transfers between devices: 148 us -> 0 us
  blocking collectives: 66.7 us -> 0 us
  starting transfers between devices: 25.7 us -> 0 us
  between operations: 14.6 us -> 0.64 us
  local copies, waits for them, and re-layouts: 4.25 us -> 13.8 us
  matrix products: 6.16 us -> 0 us
  other arithmetic: 5.75 us -> 0 us
    pallas_call x2 -> x1, Pallas kernels: 34 us -> 248 us  [line_body(): pl.pallas_call(functools.partial(move_kernel, (planes, cores, cols, piece...]
    all_to_all x6 -> x0, waiting for transfers between devices: 69.6 us -> none  [the longest x2 53.2 us: collect(): return lax.all_to_all(planes, 'tp', split_axis=0, concat_axis=0, tiled=True)]
    all_gather x3 -> x0, waiting for transfers between devices: 69.6 us -> none  [the longest x2 67.4 us: collect(): lax.all_gather(rows[None], 'rep', axis=0, tiled=True, axis_index_groups=g...]
    all_gather x3 -> x0, blocking collectives: 40.5 us -> none  [the longest x1 16.7 us: body(): attention_all = lax.all_gather(own_all, 'rep', axis=0, tiled=True)]
    all_to_all x6 -> x0, starting transfers between devices: 25.6 us -> none  [the longest x2 9.91 us: collect(): return lax.all_to_all(planes, 'tp', split_axis=0, concat_axis=0, tiled=True)]
    unnamed x1 -> x0, blocking collectives: 16 us -> none
    all_to_all x1 -> x0, blocking collectives: 10.2 us -> none  [scatter_rows(): lax.all_to_all(wide, 'rep', split_axis=0, concat_axis=0, tiled=True)]
    unnamed x23 -> x5, local copies, waits for them, and re-layouts: 2.05 us -> 11.2 us
  transfers between devices with their start and end apart: 11 -> 0, of which waited for: 7 -> 0; matrix products, arithmetic and copies ran while one was open for 4% -> 0% of each run, Pallas kernels for 7% -> 0%
where the time goes in v1:
time: 263 us
  Pallas kernels  248 us (94%)
  local copies, waits for them, and re-layouts  13.8 us (5%)
    pallas_call x1, Pallas kernels, line_body(): pl.pallas_call(functools.partial(move_kernel, (planes, cores, cols, piece...  248 us
    unnamed x5, local copies, waits for them, and re-layouts  11.2 us

profile of v1, /device:TPU:0, one launch (start us, length us, event | category | flops | bytes accessed | tf_op | source)
XLA Modules:
  0.0 262.9 jit_solution(4945600044653233949)
XLA Ops:
  0.6 1.3 broadcast_in_dim.7.post_ref
  1.9 1.3 broadcast_in_dim.6.gain_ref
  3.3 248.5 %move.1 = (bf16[4608,2048]{1,0:T(8,128)(2,1)S(1)}, bf16[1024,4608]{1,0:T(8,128)(2,1)S(1)}, bf16[4,1152]{1,0:T(4,128)(2,1)}) custom-call(bf16[128,4608]{1,0:T(8,128)(2,1)} %q_ref.1, bf16[64,4608]{1,0:T(8,128)(2,1)} %k_ref.1, bf16[64,4608]{1,0:T(8,128)(2,1)} %v_ref.1, bf16[144,4096]{1,0:T(8,128)(2,1)} %o_ref.1, bf16[4,4608]{1,0:T(4,128)(2,1)} %hidden_ref.1, ...), custom_call_target="tpu_custom_call" | custom-call | tf_op jit(solution)/shard_map/move/pallas_call | solution.py:667
  251.7 6.9 %copy.17 = bf16[4608,2048]{1,0:T(8,128)(2,1)} copy(bf16[4608,2048]{1,0:T(8,128)(2,1)S(1)} %get-tuple-element.3) | data formatting | bytes 37748736
  258.6 0.0 copy-start
  258.6 3.7 %copy.18 = bf16[1024,4608]{1,0:T(8,128)(2,1)} copy(bf16[1024,4608]{1,0:T(8,128)(2,1)S(1)} %get-tuple-element.4) | data formatting | bytes 18874368
  262.3 0.0 copy-done
  262.3 0.6 copy.19
Async XLA Ops:
  258.6 3.7 %copy-start = (bf16[4,1152]{1,0:T(4,128)(2,1)S(1)}, bf16[4,1152]{1,0:T(4,128)(2,1)}, u32[]{:S(2)}) copy-start(bf16[4,1152]{1,0:T(4,128)(2,1)} %get-tuple-element.11) | copy-start | bytes 27652

commit v2 on v1

--- a/solution.py
+++ b/solution.py
@@ -206,8 +206,8 @@
     joined, heads, result,
     stage, q_own, kv_own, o_rows,
     hidden, positions, keys, values, gain, post, freq,
-    fresh, q_heads, k_heads, v_heads, attended, partial, others, squares, squares_in,
-    early_sems, share_send, share_recv, square_send, square_recv,
+    fresh, q_heads, k_heads, v_heads, attended, partial, partial_sum, others,
+    early_sems, share_send, share_recv,
     local_sems, kv_sems, rows_send, rows_recv,
     line_send, line_recv, plane_send, plane_recv,
     twin_send, twin_recv, twin_wo_send, twin_wo_recv,
@@ -346,7 +346,7 @@
             copy.wait()
         wide = hidden[...].astype(f32)
         mean_square = jnp.mean(wide * wide, axis=-1, keepdims=True)
-        normed = (wide * lax.rsqrt(mean_square + 1e-06) * gain[...]).astype(bf16)
+        normed = (wide * lax.rsqrt(mean_square + 1e-06) * gain[...].reshape(1, -1)).astype(bf16)
 
         def columns(i, carry):
             span = pl.ds(pl.multiple_of(i * 256, 256), 256)
@@ -405,45 +405,48 @@
             for n in range(q_local):
                 attended[b : b + 1, n * head_dim : (n + 1) * head_dim] = mixed[n : n + 1]
 
-    def share_copy(p, device):
-        return remote(partial.at[p], others.at[t], share_send.at[p], share_recv.at[t], device)
-
-    def square_copy(p):
-        return remote(squares, squares_in.at[t], square_send.at[p], square_recv.at[t], at(z, c, p))
+    far_end = jnp.where(2 * z < planes, planes - 1, 0)
+
+    def share_copy(zz, dt):
+        p = lax.rem(t + dt, cols)
+        return remote(partial.at[zz], others.at[zz, t], share_send.at[zz, dt], share_recv.at[zz, t], at(z, c, p))
+
+    def share_arrival(zz, dt):
+        p = lax.rem(t + dt, cols)
+        view = others.at[zz, p]
+        return remote(view, view, share_send.at[zz, dt], share_recv.at[zz, p], at(z, c, p))
+
+    def add_slice(zz):
+        for j in range(moving, total):
+            twin_wo_copy(zz, j, other).wait_recv()
+        narrow = attended[...].astype(bf16)
+        span = pl.ds(pl.multiple_of(zz * block, 128), block)
+        partial[zz] = jnp.dot(narrow, heads[:, span], preferred_element_type=f32)
+        for dt in range(1, cols):
+            share_copy(zz, dt).start()
+
+    def sum_slice(zz):
+        share = partial[zz]
+        for dt in range(1, cols):
+            share_arrival(zz, dt).wait_recv()
+            share = share + others[zz, lax.rem(t + dt, cols)]
+        partial_sum[zz] = share
+        return jnp.sum(share * share, axis=-1, keepdims=True)
+
+    def near(step):
+        return lax.rem(far_end + 1 + step, planes)
 
     def finish():
-        narrow = attended[...].astype(bf16)
-
-        def slices(p, carry):
-            span = pl.ds(pl.multiple_of(p * block, 128), block)
-            partial[p] = jnp.dot(narrow, heads[:, span], preferred_element_type=f32)
-            return carry
-
-        lax.fori_loop(0, cols, slices, 0)
-        for dt in range(1, cols):
-            p = lax.rem(t + dt, cols)
-            share_copy(p, at(z, c, p)).start()
-        share = partial[t]
-        for dt in range(1, cols):
-            p = lax.rem(t + dt, cols)
-            remote(others.at[p], others.at[p], share_send.at[p], share_recv.at[p], at(z, c, p)).wait_recv()
-            share = share + others[p]
-        square = jnp.sum(share * share, axis=-1, keepdims=True)
-        squares[...] = jnp.broadcast_to(square, squares.shape)
-        for dt in range(1, cols):
-            square_copy(lax.rem(t + dt, cols)).start()
-        total_square = square
-        for dt in range(1, cols):
-            p = lax.rem(t + dt, cols)
-            remote(squares_in.at[p], squares_in.at[p], square_send.at[p], square_recv.at[p],
-                   at(z, c, p)).wait_recv()
-            total_square = total_square + squares_in[p][:, :1]
-        multiplier = lax.rsqrt(total_square / width + 1e-06)
-        result[...] = (share * multiplier * post[...]).astype(result.dtype)
-        for dt in range(1, cols):
-            p = lax.rem(t + dt, cols)
-            share_copy(p, at(z, c, p)).wait_send()
-            square_copy(p).wait_send()
+        add_slice(far_end)
+        square = jnp.zeros((batch, 1), f32)
+        for step in range(planes - 1):
+            square = square + sum_slice(near(step))
+        square = square + sum_slice(far_end)
+        multiplier = lax.rsqrt(square / width + 1e-06)
+        result[...] = (partial_sum[t] * multiplier * post[...].reshape(1, -1)).astype(result.dtype)
+        for zz in range(planes):
+            for dt in range(1, cols):
+                share_copy(zz, dt).wait_send()
 
     def prepare(j):
         @pl.when(j < pieces)
@@ -521,7 +524,6 @@
         copy.start()
     load_q.wait()
     prepare(jnp.int32(0))
-    prepare(jnp.int32(1))
     n_line = (z > 0).astype(jnp.int32) + (z < planes - 1).astype(jnp.int32)
     pl.semaphore_wait(barrier, len(peers) + n_line)
 
@@ -542,16 +544,16 @@
             def _():
                 give_k.start()
 
-        @pl.when(r == 1)
+        @pl.when(r == 3)
         def _():
             for dc, dt in peers:
                 rows_copy(dc, dt).start()
             for copy in early[5:]:
                 copy.start()
 
-        @pl.when(r + 2 < total)
-        def _():
-            prepare(r + 2)
+        @pl.when(r + 1 < total)
+        def _():
+            prepare(r + 1)
 
         for k in range(1, planes):
             for way in (0, 1):
@@ -590,14 +592,10 @@
             twin_copy(slot(tt, j, other), tt, j, other).wait_recv()
         return carry
 
-    lax.fori_loop(0, total + planes - 1, rounds, 0)
-
-    def twin_wo_in(j, carry):
-        for zz in range(planes):
-            twin_wo_copy(zz, j, other).wait_recv()
-        return carry
-
-    lax.fori_loop(moving, total, twin_wo_in, 0)
+    lax.fori_loop(0, total + planes - 2, rounds, 0)
+    for step in range(planes - 1):
+        add_slice(near(step))
+    rounds(jnp.int32(total + planes - 2), 0)
     finish()
 
     def sent(j, carry):
@@ -670,7 +668,7 @@
         out_shape=[
             pltpu.VMEM((width, columns), bf),
             pltpu.VMEM((features, model), bf),
-            jax.ShapeDtypeStruct((hidden.shape[0], post_gain.shape[0]), bf),
+            pltpu.VMEM((hidden.shape[0], post_gain.shape[0]), bf),
         ],
         out_specs=[pl.BlockSpec(memory_space=pltpu.VMEM)] * 3,
         scratch_shapes=[
@@ -680,25 +678,45 @@
             pltpu.VMEM((cores * cols * o_own, features // cores), bf),
             pltpu.VMEM(hidden.shape, bf), pltpu.SMEM(positions.shape, jnp.int32),
             pltpu.VMEM(key_cache.shape, bf), pltpu.VMEM(value_cache.shape, bf),
-            pltpu.VMEM((1, width), f32), pltpu.VMEM((1, share), f32), pltpu.VMEM((1, head_dim), f32),
+            pltpu.VMEM((width,), f32), pltpu.VMEM((share,), f32), pltpu.VMEM((1, head_dim), f32),
             pltpu.VMEM((batch, columns), f32), pltpu.VMEM((batch, q_local, head_dim), f32),
             pltpu.VMEM((batch, q_local, head_dim), f32), pltpu.VMEM((batch, q_local, head_dim), f32),
-            pltpu.VMEM((batch, features), f32), pltpu.VMEM((cols, batch, share), f32),
-            pltpu.VMEM((cols, batch, share), f32), pltpu.VMEM((batch, 128), f32),
-            pltpu.VMEM((cols, batch, 128), f32),
-            dma((7,)), dma((cols,)), dma((cols,)), dma((cols,)), dma((cols,)),
+            pltpu.VMEM((batch, features), f32), pltpu.VMEM((planes, batch, share), f32),
+            pltpu.VMEM((planes, batch, share), f32), pltpu.VMEM((planes, cols, batch, share), f32),
+            dma((7,)), dma((planes, cols)), dma((planes, cols)),
             dma((3,)), dma((2,)), dma((cores * cols,)), dma((cores * cols,)),
             dma((2, planes, total)), dma((planes, total)), dma((planes, moving)), dma((cols, moving)),
             dma((cols, moving)), dma((cols, moving)), dma((planes, pieces)), dma((planes, pieces)),
         ],
         compiler_params=pltpu.CompilerParams(
-            collective_id=0, has_side_effects=True, vmem_limit_bytes=VLIM),
+            collective_id=0, has_side_effects=True, vmem_limit_bytes=34 * 2**20),
         name="move",
     )(q_proj, k_proj, v_proj, o_proj, hidden, positions, key_cache, value_cache,
-      norm_gain[None], post_gain[None], freq)
-    return tuple(out)
-
-VLIM = 34 * 2**20
+      norm_gain, post_gain, freq)
+    joined, heads, result = out
+
+    def spill_kernel(a, b, r, a_out, b_out, r_out, sems):
+        copies = [pltpu.make_async_copy(r, r_out, sems.at[0])]
+        for source, target in ((a, a_out), (b, b_out)):
+            rows = source.shape[0] // 4
+            for i in range(4):
+                span = pl.ds(i * rows, rows)
+                copies.append(pltpu.make_async_copy(source.at[span], target.at[span], sems.at[len(copies)]))
+        for copy in copies:
+            copy.start()
+        for copy in copies:
+            copy.wait()
+
+    vmem = pl.BlockSpec(memory_space=pltpu.VMEM)
+    return tuple(pl.pallas_call(
+        spill_kernel,
+        in_specs=[vmem] * 3,
+        out_specs=[hbm] * 3,
+        out_shape=[jax.ShapeDtypeStruct(x.shape, x.dtype) for x in (joined, heads, result)],
+        scratch_shapes=[dma((9,))],
+        compiler_params=pltpu.CompilerParams(vmem_limit_bytes=2**20),
+        name="spill",
+    )(joined, heads, result))
 
 
 def body(*args):

time: 263 us -> 252 us (0.958)
  local copies, waits for them, and re-layouts: 13.8 us -> 0 us
  Pallas kernels: 248 us -> 251 us
    unnamed x5 -> x0, local copies, waits for them, and re-layouts: 11.2 us -> none
    pallas_call x0 -> x1, Pallas kernels: none -> 9.43 us  [line_body(): pl.pallas_call(spill_kernel, in_specs=[vmem] * 3, out_specs=[hbm] * 3, ou...]
    pallas_call x1, Pallas kernels: 248 us -> 242 us  [line_body(): pl.pallas_call(functools.partial(move_kernel, (planes, cores, cols, piece...]
    broadcast_in_dim x2 -> x0, local copies, waits for them, and re-layouts: 2.64 us -> none  [the longest x1 1.35 us: line_body(): norm_gain[None]]
where the time goes in v2:
time: 252 us
  Pallas kernels  251 us (100%)
    pallas_call x1, Pallas kernels, line_body(): pl.pallas_call(functools.partial(move_kernel, (planes, cores, cols, piece...  242 us
    pallas_call x1, Pallas kernels, line_body(): pl.pallas_call(spill_kernel, in_specs=[vmem] * 3, out_specs=[hbm] * 3, ou...  9.43 us

profile of v2, /device:TPU:0, one launch (start us, length us, event | category | flops | bytes accessed | tf_op | source)
XLA Modules:
  0.0 251.8 jit_solution(13626888029041870287)
XLA Ops:
  0.6 241.7 %move.1 = (bf16[4608,2048]{1,0:T(8,128)(2,1)S(1)}, bf16[1024,4608]{1,0:T(8,128)(2,1)S(1)}, bf16[4,1152]{1,0:T(4,128)(2,1)S(1)}) custom-call(bf16[128,4608]{1,0:T(8,128)(2,1)} %q_ref.1, bf16[64,4608]{1,0:T(8,128)(2,1)} %k_ref.1, bf16[64,4608]{1,0:T(8,128)(2,1)} %v_ref.1, bf16[144,4096]{1,0:T(8,128)(2,1)} %o_ref.1, bf16[4,4608]{1,0:T(4,128)(2,1)} %hidden_ref.1, ...), custom_call_target="tpu_custom_call" | custom-call | tf_op jit(solution)/shard_map/move/pallas_call | solution.py:665
  242.3 9.4 %spill.1 = (bf16[4608,2048]{1,0:T(8,128)(2,1)}, bf16[1024,4608]{1,0:T(8,128)(2,1)}, bf16[4,1152]{1,0:T(4,128)(2,1)}) custom-call(bf16[4608,2048]{1,0:T(8,128)(2,1)S(1)} %get-tuple-element.6.a, bf16[1024,4608]{1,0:T(8,128)(2,1)S(1)} %get-tuple-element.7.b, bf16[4,1152]{1,0:T(4,128)(2,1)S(1)} %get-tuple-element.8.r), custom_call_target="tpu_custom_call" | custom-call | tf_op jit(solution)/shard_map/spill/pallas_call | solution.py:711

commit v3 on v2

--- a/solution.py
+++ b/solution.py
@@ -255,27 +255,26 @@
         )
 
     def line_copy(zz, j, way, device):
-        return remote(stage.at[zz, j], stage.at[zz, j], line_send.at[way, zz, j],
+        return remote(stage.at[zz, j], stage.at[zz, j], line_send.at[way],
                       line_recv.at[zz, j], device)
 
     def line_wo_copy(zz, j, way, device):
-        return remote(wo_slot(zz, j, c), wo_slot(zz, j, c), line_send.at[way, zz, j],
+        return remote(wo_slot(zz, j, c), wo_slot(zz, j, c), line_send.at[way],
                       line_recv.at[zz, j], device)
 
     def plane_copy(zz, j):
-        return remote(stage.at[zz, j], slot(t, j, c), plane_send.at[zz, j],
-                      plane_recv.at[t, j], at(z, c, zz))
-
-    def plane_arrival(tt, j):
-        return remote(slot(tt, j, c), slot(tt, j, c), plane_send.at[0, j],
-                      plane_recv.at[tt, j], at(z, c, tt))
+        return remote(stage.at[zz, j], slot(t, j, c), plane_send.at[0],
+                      plane_recv.at[j], at(z, c, zz))
+
+    def wait_bytes(view, sem):
+        pltpu.make_async_copy(view, view, sem).wait()
 
     def twin_copy(src, tt, j, cc):
-        return remote(src, slot(tt, j, cc), twin_send.at[tt, j], twin_recv.at[tt, j], at(z, other, t))
+        return remote(src, slot(tt, j, cc), twin_send.at[0], twin_recv.at[0], at(z, other, t))
 
     def twin_wo_copy(zz, j, cc):
-        return remote(wo_slot(zz, j, cc), wo_slot(zz, j, cc), twin_wo_send.at[zz, j - moving],
-                      twin_wo_recv.at[zz, j - moving], at(z, other, t))
+        return remote(wo_slot(zz, j, cc), wo_slot(zz, j, cc), twin_wo_send.at[0],
+                      twin_wo_recv.at[zz], at(z, other, t))
 
     def rows_copy(dc, dt):
         cc, tt = lax.rem(c + dc, cores), lax.rem(t + dt, cols)
@@ -283,14 +282,7 @@
         src_at = pl.multiple_of((tt * cores + cc) * half, 128)
         dst_at = pl.multiple_of(mine * o_own, 16)
         return remote(o_ref.at[:, pl.ds(src_at, half)], o_rows.at[pl.ds(dst_at, o_own), :],
-                      rows_send.at[dc * cols + dt], rows_recv.at[mine], at(z, cc, tt))
-
-    def rows_arrival(dc, dt):
-        cc, tt = lax.rem(c + dc, cores), lax.rem(t + dt, cols)
-        theirs = cc * cols + tt
-        dst_at = pl.multiple_of(theirs * o_own, 16)
-        view = o_rows.at[pl.ds(dst_at, o_own), :]
-        return remote(view, view, rows_send.at[dc * cols + dt], rows_recv.at[theirs], at(z, cc, tt))
+                      rows_send.at[0], rows_recv.at[0], at(z, cc, tt))
 
     peers = [(dc, dt) for dc in range(cores) for dt in range(cols) if dc or dt]
 
@@ -409,16 +401,12 @@
 
     def share_copy(zz, dt):
         p = lax.rem(t + dt, cols)
-        return remote(partial.at[zz], others.at[zz, t], share_send.at[zz, dt], share_recv.at[zz, t], at(z, c, p))
-
-    def share_arrival(zz, dt):
-        p = lax.rem(t + dt, cols)
-        view = others.at[zz, p]
-        return remote(view, view, share_send.at[zz, dt], share_recv.at[zz, p], at(z, c, p))
+        return remote(partial.at[zz], others.at[zz, t], share_send.at[0], share_recv.at[zz], at(z, c, p))
 
     def add_slice(zz):
-        for j in range(moving, total):
-            twin_wo_copy(zz, j, other).wait_recv()
+        row = pl.multiple_of(other * half, 128)
+        col = pl.multiple_of(zz * block, 128)
+        wait_bytes(heads.at[pl.ds(row, half), pl.ds(col, block)], twin_wo_recv.at[zz])
         narrow = attended[...].astype(bf16)
         span = pl.ds(pl.multiple_of(zz * block, 128), block)
         partial[zz] = jnp.dot(narrow, heads[:, span], preferred_element_type=f32)
@@ -427,8 +415,8 @@
 
     def sum_slice(zz):
         share = partial[zz]
+        wait_bytes(others.at[0, pl.ds(0, cols - 1)], share_recv.at[zz])
         for dt in range(1, cols):
-            share_arrival(zz, dt).wait_recv()
             share = share + others[zz, lax.rem(t + dt, cols)]
         partial_sum[zz] = share
         return jnp.sum(share * share, axis=-1, keepdims=True)
@@ -444,9 +432,7 @@
         square = square + sum_slice(far_end)
         multiplier = lax.rsqrt(square / width + 1e-06)
         result[...] = (partial_sum[t] * multiplier * post[...].reshape(1, -1)).astype(result.dtype)
-        for zz in range(planes):
-            for dt in range(1, cols):
-                share_copy(zz, dt).wait_send()
+        wait_bytes(others.at[pl.ds(0, cols - 1)], share_send.at[0])
 
     def prepare(j):
         @pl.when(j < pieces)
@@ -474,8 +460,7 @@
         @pl.when(j == moving)
         def _():
             load_o.wait()
-            for dc, dt in peers:
-                rows_arrival(dc, dt).wait_recv()
+            wait_bytes(o_rows.at[pl.ds(0, len(peers) * o_own)], rows_recv.at[0])
 
         @pl.when(jnp.logical_and(j >= moving, j < total))
         def _():
@@ -572,24 +557,19 @@
 
         @pl.when(jnp.logical_and(j >= 0, j < moving))
         def _():
+            wait_bytes(stage.at[0, pl.ds(0, cols - 1)], plane_recv.at[j])
             for dt in range(1, cols):
                 tt = lax.rem(t + dt, cols)
-                plane_arrival(tt, j).wait_recv()
                 twin_copy(slot(tt, j, c), tt, j, c).start()
 
         @pl.when(r == moving + 1 + far)
         def _():
-            lax.fori_loop(0, moving, twin_in, 0)
+            wait_bytes(joined.at[pl.ds(0, width // cores)], twin_recv.at[0])
             project()
 
         @pl.when(r == moving + 2 + far)
         def _():
             attend()
-        return carry
-
-    def twin_in(j, carry):
-        for tt in range(cols):
-            twin_copy(slot(tt, j, other), tt, j, other).wait_recv()
         return carry
 
     lax.fori_loop(0, total + planes - 2, rounds, 0)
@@ -598,38 +578,17 @@
     rounds(jnp.int32(total + planes - 2), 0)
     finish()
 
-    def sent(j, carry):
-        for zz in range(planes):
-            for way in (0, 1):
-                room = z > 0 if way == 0 else z < planes - 1
-                passes = z <= zz if way == 0 else z >= zz
-
-                @pl.when(jnp.logical_and(room, passes))
-                def _():
-                    @pl.when(j < moving)
-                    def _():
-                        line_copy(zz, j, way, at(z, other, t)).wait_send()
-
-                    @pl.when(j >= moving)
-                    def _():
-                        line_wo_copy(zz, j, way, at(z, other, t)).wait_send()
-
-            @pl.when(jnp.logical_and(j < moving, t != zz))
+    unit = deep * 128 // joined.shape[1]
+    for way, count in ((0, planes - z), (1, z + 1)):
+        for m in range(1, planes):
+
+            @pl.when(count == m)
             def _():
-                plane_copy(zz, j).wait_send()
-
-            @pl.when(j < moving)
-            def _():
-                twin_copy(slot(zz, j, c), zz, j, c).wait_send()
-
-            @pl.when(j >= moving)
-            def _():
-                twin_wo_copy(zz, j, c).wait_send()
-        return carry
-
-    lax.fori_loop(0, total, sent, 0)
-    for dc, dt in peers:
-        rows_copy(dc, dt).wait_send()
+                wait_bytes(joined.at[pl.ds(0, m * total * unit)], line_send.at[way])
+    wait_bytes(joined.at[pl.ds(0, (planes - 1) * moving * unit)], plane_send.at[0])
+    wait_bytes(joined.at[pl.ds(0, width // cores)], twin_send.at[0])
+    wait_bytes(heads.at[pl.ds(0, half)], twin_wo_send.at[0])
+    wait_bytes(o_rows.at[pl.ds(0, len(peers) * o_own)], rows_send.at[0])
 
     @pl.when(even)
     def _():
@@ -683,10 +642,10 @@
             pltpu.VMEM((batch, q_local, head_dim), f32), pltpu.VMEM((batch, q_local, head_dim), f32),
             pltpu.VMEM((batch, features), f32), pltpu.VMEM((planes, batch, share), f32),
             pltpu.VMEM((planes, batch, share), f32), pltpu.VMEM((planes, cols, batch, share), f32),
-            dma((7,)), dma((planes, cols)), dma((planes, cols)),
-            dma((3,)), dma((2,)), dma((cores * cols,)), dma((cores * cols,)),
-            dma((2, planes, total)), dma((planes, total)), dma((planes, moving)), dma((cols, moving)),
-            dma((cols, moving)), dma((cols, moving)), dma((planes, pieces)), dma((planes, pieces)),
+            dma((7,)), dma((1,)), dma((planes,)),
+            dma((3,)), dma((2,)), dma((1,)), dma((1,)),
+            dma((2,)), dma((planes, total)), dma((1,)), dma((moving,)),
+            dma((1,)), dma((1,)), dma((1,)), dma((planes,)),
         ],
         compiler_params=pltpu.CompilerParams(
             collective_id=0, has_side_effects=True, vmem_limit_bytes=34 * 2**20),

time: 252 us -> 249 us (0.988)
  Pallas kernels: 251 us -> 248 us
    pallas_call x1, Pallas kernels: 242 us -> 239 us  [line_body(): pl.pallas_call(functools.partial(move_kernel, (planes, cores, cols, piece...]
where the time goes in v3:
time: 249 us
  Pallas kernels  248 us (100%)
    pallas_call x1, Pallas kernels, line_body(): pl.pallas_call(functools.partial(move_kernel, (planes, cores, cols, piece...  239 us
    pallas_call x1, Pallas kernels, line_body(): pl.pallas_call(spill_kernel, in_specs=[vmem] * 3, out_specs=[hbm] * 3, ou...  9.43 us

profile of v3, /device:TPU:0, one launch (start us, length us, event | category | flops | bytes accessed | tf_op | source)
XLA Modules:
  0.0 248.6 jit_solution(7159576753022232348)
XLA Ops:
  0.6 238.5 %move.1 = (bf16[4608,2048]{1,0:T(8,128)(2,1)S(1)}, bf16[1024,4608]{1,0:T(8,128)(2,1)S(1)}, bf16[4,1152]{1,0:T(4,128)(2,1)S(1)}) custom-call(bf16[128,4608]{1,0:T(8,128)(2,1)} %q_ref.1, bf16[64,4608]{1,0:T(8,128)(2,1)} %k_ref.1, bf16[64,4608]{1,0:T(8,128)(2,1)} %v_ref.1, bf16[144,4096]{1,0:T(8,128)(2,1)} %o_ref.1, bf16[4,4608]{1,0:T(4,128)(2,1)} %hidden_ref.1, ...), custom_call_target="tpu_custom_call" | custom-call | tf_op jit(solution)/shard_map/move/pallas_call | solution.py:624
  239.2 9.4 %spill.1 = (bf16[4608,2048]{1,0:T(8,128)(2,1)}, bf16[1024,4608]{1,0:T(8,128)(2,1)}, bf16[4,1152]{1,0:T(4,128)(2,1)}) custom-call(bf16[4608,2048]{1,0:T(8,128)(2,1)S(1)} %get-tuple-element.6.a, bf16[1024,4608]{1,0:T(8,128)(2,1)S(1)} %get-tuple-element.7.b, bf16[4,1152]{1,0:T(4,128)(2,1)S(1)} %get-tuple-element.8.r), custom_call_target="tpu_custom_call" | custom-call | tf_op jit(solution)/shard_map/spill/pallas_call | solution.py:670

commit v4 on v3

--- a/solution.py
+++ b/solution.py
@@ -206,8 +206,8 @@
     joined, heads, result,
     stage, q_own, kv_own, o_rows,
     hidden, positions, keys, values, gain, post, freq,
-    fresh, q_heads, k_heads, v_heads, attended, partial, partial_sum, others,
-    early_sems, share_send, share_recv,
+    fresh, q_heads, k_heads, v_heads, attended, far_attended, far_partial, partial, partial_sum, others,
+    early_sems, far_sems, share_send, share_recv,
     local_sems, kv_sems, rows_send, rows_recv,
     line_send, line_recv, plane_send, plane_recv,
     twin_send, twin_recv, twin_wo_send, twin_wo_recv,
@@ -299,6 +299,13 @@
     @pl.when(z < planes - 1)
     def _():
         pl.semaphore_signal(barrier, inc=1, device_id=at(z + 1, c, t), device_id_type=MESH)
+
+    far_end = jnp.where(2 * z < planes, planes - 1, 0)
+    is_end = jnp.logical_or(z == 0, z == planes - 1)
+
+    @pl.when(is_end)
+    def _():
+        pl.semaphore_signal(barrier, inc=1, device_id=at(far_end, c, t), device_id_type=MESH)
 
     load_q = pltpu.make_async_copy(q_ref, q_own, local_sems.at[0])
     load_q.start()
@@ -397,21 +404,38 @@
             for n in range(q_local):
                 attended[b : b + 1, n * head_dim : (n + 1) * head_dim] = mixed[n : n + 1]
 
-    far_end = jnp.where(2 * z < planes, planes - 1, 0)
-
     def share_copy(zz, dt):
         p = lax.rem(t + dt, cols)
         return remote(partial.at[zz], others.at[zz, t], share_send.at[0], share_recv.at[zz], at(z, c, p))
 
-    def add_slice(zz):
+    def take_heads(zz):
         row = pl.multiple_of(other * half, 128)
         col = pl.multiple_of(zz * block, 128)
         wait_bytes(heads.at[pl.ds(row, half), pl.ds(col, block)], twin_wo_recv.at[zz])
-        narrow = attended[...].astype(bf16)
+
+    def project_slice(source, zz):
         span = pl.ds(pl.multiple_of(zz * block, 128), block)
-        partial[zz] = jnp.dot(narrow, heads[:, span], preferred_element_type=f32)
+        return jnp.dot(source[...].astype(bf16), heads[:, span], preferred_element_type=f32)
+
+    def answer_far():
+        ask_far.wait_recv()
+        take_heads(z)
+        far_partial[...] = project_slice(far_attended, z)
+        tell_far.start()
+        partial[z] = project_slice(attended, z)
+        share_out(z)
+
+    def share_out(zz):
         for dt in range(1, cols):
             share_copy(zz, dt).start()
+
+    def add_slice(zz):
+        take_heads(zz)
+        partial[zz] = project_slice(attended, zz)
+        share_out(zz)
+
+    ask_far = remote(attended, far_attended, far_sems.at[0], far_sems.at[1], at(far_end, c, t))
+    tell_far = remote(far_partial, partial.at[z], far_sems.at[2], far_sems.at[3], at(far_end, c, t))
 
     def sum_slice(zz):
         share = partial[zz]
@@ -425,7 +449,6 @@
         return lax.rem(far_end + 1 + step, planes)
 
     def finish():
-        add_slice(far_end)
         square = jnp.zeros((batch, 1), f32)
         for step in range(planes - 1):
             square = square + sum_slice(near(step))
@@ -509,7 +532,7 @@
         copy.start()
     load_q.wait()
     prepare(jnp.int32(0))
-    n_line = (z > 0).astype(jnp.int32) + (z < planes - 1).astype(jnp.int32)
+    n_line = (z > 0).astype(jnp.int32) + (z < planes - 1).astype(jnp.int32) + is_end.astype(jnp.int32)
     pl.semaphore_wait(barrier, len(peers) + n_line)
 
     def rounds(r, carry):
@@ -541,6 +564,8 @@
             prepare(r + 1)
 
         for k in range(1, planes):
+            if k == planes - 1:
+                pl.when(jnp.logical_and(is_end, r == total + planes - 3))(answer_far)
             for way in (0, 1):
                 zz = z + k if way == 0 else z - k
                 j = r - k
@@ -566,17 +591,38 @@
         def _():
             wait_bytes(joined.at[pl.ds(0, width // cores)], twin_recv.at[0])
             project()
-
-        @pl.when(r == moving + 2 + far)
-        def _():
             attend()
+
+            @pl.when(is_end)
+            def _():
+                ask_far.start()
+
         return carry
 
     lax.fori_loop(0, total + planes - 2, rounds, 0)
-    for step in range(planes - 1):
-        add_slice(near(step))
+
+    @pl.when(is_end)
+    def _():
+        for k in range(1, planes - 1):
+            add_slice(jnp.where(z == 0, k, planes - 1 - k))
+        remote(partial.at[far_end], partial.at[far_end], far_sems.at[2], far_sems.at[3],
+               at(far_end, c, t)).wait_recv()
+        share_out(far_end)
+
     rounds(jnp.int32(total + planes - 2), 0)
+
+    @pl.when(jnp.logical_not(is_end))
+    def _():
+        for zz in range(planes):
+            add_slice(zz)
+
     finish()
+
+    @pl.when(is_end)
+    def _():
+        take_heads(far_end)
+        ask_far.wait_send()
+        tell_far.wait_send()
 
     unit = deep * 128 // joined.shape[1]
     for way, count in ((0, planes - z), (1, z + 1)):
@@ -640,9 +686,10 @@
             pltpu.VMEM((width,), f32), pltpu.VMEM((share,), f32), pltpu.VMEM((1, head_dim), f32),
             pltpu.VMEM((batch, columns), f32), pltpu.VMEM((batch, q_local, head_dim), f32),
             pltpu.VMEM((batch, q_local, head_dim), f32), pltpu.VMEM((batch, q_local, head_dim), f32),
-            pltpu.VMEM((batch, features), f32), pltpu.VMEM((planes, batch, share), f32),
+            pltpu.VMEM((batch, features), f32), pltpu.VMEM((batch, features), f32),
+            pltpu.VMEM((batch, share), f32), pltpu.VMEM((planes, batch, share), f32),
             pltpu.VMEM((planes, batch, share), f32), pltpu.VMEM((planes, cols, batch, share), f32),
-            dma((7,)), dma((1,)), dma((planes,)),
+            dma((7,)), dma((4,)), dma((1,)), dma((planes,)),
             dma((3,)), dma((2,)), dma((1,)), dma((1,)),
             dma((2,)), dma((planes, total)), dma((1,)), dma((moving,)),
             dma((1,)), dma((1,)), dma((1,)), dma((planes,)),
@@ -685,6 +732,7 @@
     fits = (
         reps == 2 * cols
         and cols % 2 == 0
+        and cols > 2
         and key_cache.shape[3] == lanes
         and q_proj.shape[0] == lanes
         and 2 * k_proj.shape[0] == lanes

time: 249 us -> 247 us (level)
  no operation moved by 1% of the time
where the time goes in v4:
time: 247 us
  Pallas kernels  246 us (100%)
    pallas_call x1, Pallas kernels, line_body(): pl.pallas_call(functools.partial(move_kernel, (planes, cores, cols, piece...  237 us
    pallas_call x1, Pallas kernels, line_body(): pl.pallas_call(spill_kernel, in_specs=[vmem] * 3, out_specs=[hbm] * 3, ou...  9.43 us

profile of v4, /device:TPU:0, one launch (start us, length us, event | category | flops | bytes accessed | tf_op | source)
XLA Modules:
  0.0 246.9 jit_solution(15770118215086737226)
XLA Ops:
  0.6 236.8 %move.1 = (bf16[4608,2048]{1,0:T(8,128)(2,1)S(1)}, bf16[1024,4608]{1,0:T(8,128)(2,1)S(1)}, bf16[4,1152]{1,0:T(4,128)(2,1)S(1)}) custom-call(bf16[128,4608]{1,0:T(8,128)(2,1)} %q_ref.1, bf16[64,4608]{1,0:T(8,128)(2,1)} %k_ref.1, bf16[64,4608]{1,0:T(8,128)(2,1)} %v_ref.1, bf16[144,4096]{1,0:T(8,128)(2,1)} %o_ref.1, bf16[4,4608]{1,0:T(4,128)(2,1)} %hidden_ref.1, ...), custom_call_target="tpu_custom_call" | custom-call | tf_op jit(solution)/shard_map/move/pallas_call | solution.py:670
  237.5 9.4 %spill.1 = (bf16[4608,2048]{1,0:T(8,128)(2,1)}, bf16[1024,4608]{1,0:T(8,128)(2,1)}, bf16[4,1152]{1,0:T(4,128)(2,1)}) custom-call(bf16[4608,2048]{1,0:T(8,128)(2,1)S(1)} %get-tuple-element.6.a, bf16[1024,4608]{1,0:T(8,128)(2,1)S(1)} %get-tuple-element.7.b, bf16[4,1152]{1,0:T(4,128)(2,1)S(1)} %get-tuple-element.8.r), custom_call_target="tpu_custom_call" | custom-call | tf_op jit(solution)/shard_map/spill/pallas_call | solution.py:717

commit v5 on v4

--- a/solution.py
+++ b/solution.py
@@ -208,7 +208,7 @@
     hidden, positions, keys, values, gain, post, freq,
     fresh, q_heads, k_heads, v_heads, attended, far_attended, far_partial, partial, partial_sum, others,
     early_sems, far_sems, share_send, share_recv,
-    local_sems, kv_sems, rows_send, rows_recv,
+    q_sems, local_sems, kv_sems, rows_send, rows_recv,
     line_send, line_recv, plane_send, plane_recv,
     twin_send, twin_recv, twin_wo_send, twin_wo_recv,
 ):
@@ -254,13 +254,16 @@
             device_id=device, device_id_type=MESH,
         )
 
-    def line_copy(zz, j, way, device):
+    def place(zz, to):
+        return zz - (zz > to).astype(jnp.int32)
+
+    def line_copy(zz, j, way, to, device):
         return remote(stage.at[zz, j], stage.at[zz, j], line_send.at[way],
-                      line_recv.at[zz, j], device)
-
-    def line_wo_copy(zz, j, way, device):
+                      line_recv.at[place(zz, to), j], device)
+
+    def line_wo_copy(zz, j, way, to, device):
         return remote(wo_slot(zz, j, c), wo_slot(zz, j, c), line_send.at[way],
-                      line_recv.at[zz, j], device)
+                      line_recv.at[place(zz, to), j], device)
 
     def plane_copy(zz, j):
         return remote(stage.at[zz, j], slot(t, j, c), plane_send.at[0],
@@ -307,8 +310,12 @@
     def _():
         pl.semaphore_signal(barrier, inc=1, device_id=at(far_end, c, t), device_id_type=MESH)
 
-    load_q = pltpu.make_async_copy(q_ref, q_own, local_sems.at[0])
-    load_q.start()
+    def load_q(j):
+        span = pl.ds(pl.multiple_of(j * deep, 128), deep)
+        return pltpu.make_async_copy(q_ref.at[:, span], q_own.at[:, span], q_sems.at[j])
+
+    for j in range(pieces):
+        load_q(j).start()
     mine = c * cols + t
     load_o = pltpu.make_async_copy(
         o_ref.at[:, pl.ds(pl.multiple_of((t * cores + c) * half, 128), half)],
@@ -460,6 +467,7 @@
     def prepare(j):
         @pl.when(j < pieces)
         def _():
+            load_q(j).wait()
             span = pl.ds(pl.multiple_of(j * deep, 128), deep)
             stage[z, j] = jnp.transpose(q_own[:, span])
 
@@ -493,25 +501,26 @@
                 o_rows[:, pl.ds(col, wo_rows)])
 
     def send_line(zz, j, way):
-        target = at(z - 1, c, t) if way == 0 else at(z + 1, c, t)
+        to = z - 1 if way == 0 else z + 1
+        target = at(to, c, t)
         room = z > 0 if way == 0 else z < planes - 1
 
         @pl.when(jnp.logical_and(room, j < moving))
         def _():
-            line_copy(zz, j, way, target).start()
+            line_copy(zz, j, way, to, target).start()
 
         @pl.when(jnp.logical_and(room, j >= moving))
         def _():
-            line_wo_copy(zz, j, way, target).start()
+            line_wo_copy(zz, j, way, to, target).start()
 
     def wait_line(zz, j):
         @pl.when(j < moving)
         def _():
-            line_copy(zz, j, 0, at(z, other, t)).wait_recv()
+            line_copy(zz, j, 0, z, at(z, other, t)).wait_recv()
 
         @pl.when(j >= moving)
         def _():
-            line_wo_copy(zz, j, 0, at(z, other, t)).wait_recv()
+            line_wo_copy(zz, j, 0, z, at(z, other, t)).wait_recv()
 
     def deliver(zz, j):
         @pl.when(jnp.logical_and(j < moving, t != zz))
@@ -530,7 +539,6 @@
 
     for copy in early[:5]:
         copy.start()
-    load_q.wait()
     prepare(jnp.int32(0))
     n_line = (z > 0).astype(jnp.int32) + (z < planes - 1).astype(jnp.int32) + is_end.astype(jnp.int32)
     pl.semaphore_wait(barrier, len(peers) + n_line)
@@ -690,8 +698,8 @@
             pltpu.VMEM((batch, share), f32), pltpu.VMEM((planes, batch, share), f32),
             pltpu.VMEM((planes, batch, share), f32), pltpu.VMEM((planes, cols, batch, share), f32),
             dma((7,)), dma((4,)), dma((1,)), dma((planes,)),
-            dma((3,)), dma((2,)), dma((1,)), dma((1,)),
-            dma((2,)), dma((planes, total)), dma((1,)), dma((moving,)),
+            dma((pieces,)), dma((3,)), dma((2,)), dma((1,)), dma((1,)),
+            dma((2,)), dma((planes - 1, total)), dma((1,)), dma((moving,)),
             dma((1,)), dma((1,)), dma((1,)), dma((planes,)),
         ],
         compiler_params=pltpu.CompilerParams(
@@ -702,16 +710,16 @@
     joined, heads, result = out
 
     def spill_kernel(a, b, r, a_out, b_out, r_out, sems):
-        copies = [pltpu.make_async_copy(r, r_out, sems.at[0])]
-        for source, target in ((a, a_out), (b, b_out)):
-            rows = source.shape[0] // 4
-            for i in range(4):
-                span = pl.ds(i * rows, rows)
-                copies.append(pltpu.make_async_copy(source.at[span], target.at[span], sems.at[len(copies)]))
-        for copy in copies:
-            copy.start()
-        for copy in copies:
-            copy.wait()
+        small = pltpu.make_async_copy(r, r_out, sems.at[0])
+        small.start()
+        for i, (source, target) in enumerate(((a, a_out), (b, b_out))):
+            rows = 32 * source.dtype.itemsize
+            for low in range(0, source.shape[0], rows):
+                span = pl.ds(low, min(rows, source.shape[0] - low))
+                pltpu.make_async_copy(source.at[span], target.at[span], sems.at[i + 1]).start()
+        small.wait()
+        for i, (source, target) in enumerate(((a, a_out), (b, b_out))):
+            pltpu.make_async_copy(source, target, sems.at[i + 1]).wait()
 
     vmem = pl.BlockSpec(memory_space=pltpu.VMEM)
     return tuple(pl.pallas_call(
@@ -719,7 +727,7 @@
         in_specs=[vmem] * 3,
         out_specs=[hbm] * 3,
         out_shape=[jax.ShapeDtypeStruct(x.shape, x.dtype) for x in (joined, heads, result)],
-        scratch_shapes=[dma((9,))],
+        scratch_shapes=[dma((3,))],
         compiler_params=pltpu.CompilerParams(vmem_limit_bytes=2**20),
         name="spill",
     )(joined, heads, result))

time: 247 us -> 247 us (level)
  no operation moved by 1% of the time
where the time goes in v5:
time: 247 us
  Pallas kernels  246 us (100%)
    pallas_call x1, Pallas kernels, line_body(): pl.pallas_call(functools.partial(move_kernel, (planes, cores, cols, piece...  237 us
    pallas_call x1, Pallas kernels, line_body(): pl.pallas_call(spill_kernel, in_specs=[vmem] * 3, out_specs=[hbm] * 3, ou...  9.27 us

profile of v5, /device:TPU:0, one launch (start us, length us, event | category | flops | bytes accessed | tf_op | source)
XLA Modules:
  0.0 246.7 jit_solution(14915369346176914234)
XLA Ops:
  0.6 236.7 %move.1 = (bf16[4608,2048]{1,0:T(8,128)(2,1)S(1)}, bf16[1024,4608]{1,0:T(8,128)(2,1)S(1)}, bf16[4,1152]{1,0:T(4,128)(2,1)S(1)}) custom-call(bf16[128,4608]{1,0:T(8,128)(2,1)} %q_ref.1, bf16[64,4608]{1,0:T(8,128)(2,1)} %k_ref.1, bf16[64,4608]{1,0:T(8,128)(2,1)} %v_ref.1, bf16[144,4096]{1,0:T(8,128)(2,1)} %o_ref.1, bf16[4,4608]{1,0:T(4,128)(2,1)} %hidden_ref.1, ...), custom_call_target="tpu_custom_call" | custom-call | tf_op jit(solution)/shard_map/move/pallas_call | solution.py:678
  237.4 9.3 %spill.1 = (bf16[4608,2048]{1,0:T(8,128)(2,1)}, bf16[1024,4608]{1,0:T(8,128)(2,1)}, bf16[4,1152]{1,0:T(4,128)(2,1)}) custom-call(bf16[4608,2048]{1,0:T(8,128)(2,1)S(1)} %get-tuple-element.6.a, bf16[1024,4608]{1,0:T(8,128)(2,1)S(1)} %get-tuple-element.7.b, bf16[4,1152]{1,0:T(4,128)(2,1)S(1)} %get-tuple-element.8.r), custom_call_target="tpu_custom_call" | custom-call | tf_op jit(solution)/shard_map/spill/pallas_call | solution.py:725

commit v6 on v5

--- a/solution.py
+++ b/solution.py
@@ -208,7 +208,7 @@
     hidden, positions, keys, values, gain, post, freq,
     fresh, q_heads, k_heads, v_heads, attended, far_attended, far_partial, partial, partial_sum, others,
     early_sems, far_sems, share_send, share_recv,
-    q_sems, local_sems, kv_sems, rows_send, rows_recv,
+    tail_sems, q_sems, local_sems, kv_sems, rows_send, rows_recv,
     line_send, line_recv, plane_send, plane_recv,
     twin_send, twin_recv, twin_wo_send, twin_wo_recv,
 ):
@@ -223,6 +223,8 @@
     block = cols * cores * o_own
     half = heads.shape[0] // cores
     wo_rows = half // pieces
+    tail_rows = 16
+    main_rows = wo_rows - tail_rows
     moving = 2 * pieces
     total = 3 * pieces
     q_all = cores * cols * q_rows
@@ -278,6 +280,23 @@
     def twin_wo_copy(zz, j, cc):
         return remote(wo_slot(zz, j, cc), wo_slot(zz, j, cc), twin_wo_send.at[0],
                       twin_wo_recv.at[zz], at(z, other, t))
+
+    def part(zz, cc, low, rows):
+        row = pl.multiple_of(cc * half + (pieces - 1) * wo_rows + low, 16)
+        return heads.at[pl.ds(row, rows), pl.ds(pl.multiple_of(zz * block, 128), block)]
+
+    def main_line(zz, way, to, device):
+        view = part(zz, c, 0, main_rows)
+        return remote(view, view, line_send.at[way], line_recv.at[place(zz, to), total - 1], device)
+
+    def tail_line(zz, way, to):
+        view = part(zz, c, main_rows, tail_rows)
+        return (remote(view, view, line_send.at[way], tail_sems.at[0], at(to, c, t)),
+                remote(view, view, tail_sems.at[2], tail_sems.at[1], at(to, other, t)))
+
+    def main_twin(zz):
+        view = part(zz, c, 0, main_rows)
+        return remote(view, view, tail_sems.at[3], twin_wo_recv.at[zz], at(z, other, t))
 
     def rows_copy(dc, dt):
         cc, tt = lax.rem(c + dc, cores), lax.rem(t + dt, cols)
@@ -306,9 +325,13 @@
     far_end = jnp.where(2 * z < planes, planes - 1, 0)
     is_end = jnp.logical_or(z == 0, z == planes - 1)
 
+    is_next = jnp.logical_or(z == 1, z == planes - 2)
+
     @pl.when(is_end)
     def _():
         pl.semaphore_signal(barrier, inc=1, device_id=at(far_end, c, t), device_id_type=MESH)
+        pl.semaphore_signal(barrier, inc=1, device_id=at(jnp.where(z == 0, 1, planes - 2), 1 - c, t),
+                            device_id_type=MESH)
 
     def load_q(j):
         span = pl.ds(pl.multiple_of(j * deep, 128), deep)
@@ -509,18 +532,33 @@
         def _():
             line_copy(zz, j, way, to, target).start()
 
-        @pl.when(jnp.logical_and(room, j >= moving))
+        ends = jnp.logical_and(j == total - 1, to == 0 if way == 0 else to == planes - 1)
+        ends = jnp.logical_and(ends, zz == planes - 1 if way == 0 else zz == 0)
+
+        @pl.when(jnp.logical_and(jnp.logical_and(room, j >= moving), jnp.logical_not(ends)))
         def _():
             line_wo_copy(zz, j, way, to, target).start()
+
+        @pl.when(jnp.logical_and(room, ends))
+        def _():
+            main_line(zz, way, to, target).start()
+            for copy in tail_line(zz, way, to):
+                copy.start()
 
     def wait_line(zz, j):
         @pl.when(j < moving)
         def _():
             line_copy(zz, j, 0, z, at(z, other, t)).wait_recv()
 
-        @pl.when(j >= moving)
+        last = jnp.logical_and(j == total - 1, jnp.logical_and(is_end, zz == far_end))
+
+        @pl.when(jnp.logical_and(j >= moving, jnp.logical_not(last)))
         def _():
             line_wo_copy(zz, j, 0, z, at(z, other, t)).wait_recv()
+
+        @pl.when(last)
+        def _():
+            main_line(zz, 0, z, at(z, other, t)).wait_recv()
 
     def deliver(zz, j):
         @pl.when(jnp.logical_and(j < moving, t != zz))
@@ -533,14 +571,20 @@
             joined[pl.ds(row, deep), pl.ds(column(t, j, c), 128)] = stage[zz, j]
             twin_copy(stage.at[zz, j], t, j, c).start()
 
-        @pl.when(j >= moving)
+        last = jnp.logical_and(j == total - 1, jnp.logical_and(is_end, zz == far_end))
+
+        @pl.when(jnp.logical_and(j >= moving, jnp.logical_not(last)))
         def _():
             twin_wo_copy(zz, j, c).start()
+
+        @pl.when(last)
+        def _():
+            main_twin(zz).start()
 
     for copy in early[:5]:
         copy.start()
     prepare(jnp.int32(0))
-    n_line = (z > 0).astype(jnp.int32) + (z < planes - 1).astype(jnp.int32) + is_end.astype(jnp.int32)
+    n_line = (z > 0).astype(jnp.int32) + (z < planes - 1).astype(jnp.int32) + is_end.astype(jnp.int32) + is_next.astype(jnp.int32)
     pl.semaphore_wait(barrier, len(peers) + n_line)
 
     def rounds(r, carry):
@@ -628,7 +672,12 @@
 
     @pl.when(is_end)
     def _():
-        take_heads(far_end)
+        row = pl.multiple_of(other * half, 128)
+        col = pl.multiple_of(far_end * block, 128)
+        wait_bytes(heads.at[pl.ds(row, half - tail_rows), pl.ds(col, block)], twin_wo_recv.at[far_end])
+        wait_bytes(part(far_end, c, main_rows, tail_rows), tail_sems.at[0])
+        wait_bytes(part(far_end, other, main_rows, tail_rows), tail_sems.at[1])
+        wait_bytes(part(far_end, c, 0, main_rows), tail_sems.at[3])
         ask_far.wait_send()
         tell_far.wait_send()
 
@@ -641,7 +690,19 @@
                 wait_bytes(joined.at[pl.ds(0, m * total * unit)], line_send.at[way])
     wait_bytes(joined.at[pl.ds(0, (planes - 1) * moving * unit)], plane_send.at[0])
     wait_bytes(joined.at[pl.ds(0, width // cores)], twin_send.at[0])
-    wait_bytes(heads.at[pl.ds(0, half)], twin_wo_send.at[0])
+
+    @pl.when(is_end)
+    def _():
+        wait_bytes(heads.at[pl.ds(0, half - wo_rows // planes)], twin_wo_send.at[0])
+
+    @pl.when(jnp.logical_not(is_end))
+    def _():
+        wait_bytes(heads.at[pl.ds(0, half)], twin_wo_send.at[0])
+
+    @pl.when(is_next)
+    def _():
+        wait_bytes(part(z, c, main_rows, tail_rows), tail_sems.at[2])
+
     wait_bytes(o_rows.at[pl.ds(0, len(peers) * o_own)], rows_send.at[0])
 
     @pl.when(even)
@@ -698,7 +759,7 @@
             pltpu.VMEM((batch, share), f32), pltpu.VMEM((planes, batch, share), f32),
             pltpu.VMEM((planes, batch, share), f32), pltpu.VMEM((planes, cols, batch, share), f32),
             dma((7,)), dma((4,)), dma((1,)), dma((planes,)),
-            dma((pieces,)), dma((3,)), dma((2,)), dma((1,)), dma((1,)),
+            dma((4,)), dma((pieces,)), dma((3,)), dma((2,)), dma((1,)), dma((1,)),
             dma((2,)), dma((planes - 1, total)), dma((1,)), dma((moving,)),
             dma((1,)), dma((1,)), dma((1,)), dma((planes,)),
         ],
@@ -740,7 +801,7 @@
     fits = (
         reps == 2 * cols
         and cols % 2 == 0
-        and cols > 2
+        and cols > 3
         and key_cache.shape[3] == lanes
         and q_proj.shape[0] == lanes
         and 2 * k_proj.shape[0] == lanes

time: 247 us -> 247 us (level)
  no operation moved by 1% of the time
where the time goes in v6:
time: 247 us; the launch traced here: 246 us
  Pallas kernels  246 us (100%)
    pallas_call x1, Pallas kernels, line_body(): pl.pallas_call(functools.partial(move_kernel, (planes, cores, cols, piece...  236 us
    pallas_call x1, Pallas kernels, line_body(): pl.pallas_call(spill_kernel, in_specs=[vmem] * 3, out_specs=[hbm] * 3, ou...  9.27 us

profile of v6, /device:TPU:0, one launch (start us, length us, event | category | flops | bytes accessed | tf_op | source)
XLA Modules:
  0.0 246.4 jit_solution(8158362424380476934)
XLA Ops:
  0.6 236.5 %move.1 = (bf16[4608,2048]{1,0:T(8,128)(2,1)S(1)}, bf16[1024,4608]{1,0:T(8,128)(2,1)S(1)}, bf16[4,1152]{1,0:T(4,128)(2,1)S(1)}) custom-call(bf16[128,4608]{1,0:T(8,128)(2,1)} %q_ref.1, bf16[64,4608]{1,0:T(8,128)(2,1)} %k_ref.1, bf16[64,4608]{1,0:T(8,128)(2,1)} %v_ref.1, bf16[144,4096]{1,0:T(8,128)(2,1)} %o_ref.1, bf16[4,4608]{1,0:T(4,128)(2,1)} %hidden_ref.1, ...), custom_call_target="tpu_custom_call" | custom-call | tf_op jit(solution)/shard_map/move/pallas_call | solution.py:739
  237.1 9.3 %spill.1 = (bf16[4608,2048]{1,0:T(8,128)(2,1)}, bf16[1024,4608]{1,0:T(8,128)(2,1)}, bf16[4,1152]{1,0:T(4,128)(2,1)}) custom-call(bf16[4608,2048]{1,0:T(8,128)(2,1)S(1)} %get-tuple-element.6.a, bf16[1024,4608]{1,0:T(8,128)(2,1)S(1)} %get-tuple-element.7.b, bf16[4,1152]{1,0:T(4,128)(2,1)S(1)} %get-tuple-element.8.r), custom_call_target="tpu_custom_call" | custom-call | tf_op jit(solution)/shard_map/spill/pallas_call | solution.py:786
